TPU v7x, 128 devices: a whole 4x4x4 slice. The times are simulated.
128 devices in a mesh: dp: 1, ep: 128 (over z, y, x, core).
Axes of the slice: x: 4, y: 4, z: 4, core: 2. Of those that a mesh axis runs over, the one named last changes fastest.
Arguments:
- x_tokens: bfloat16 [8192, 1536], P(('dp', 'ep'))
- slot_expert: int32 [128], replicated
- w1_slots: bfloat16 [128, 1536, 512], P('ep')
- w3_slots: bfloat16 [128, 1536, 512], P('ep')
- w2_slots: bfloat16 [128, 512, 1536], P('ep')
- assign: int32 [8192, 6], P(('dp', 'ep'))
- w_router: bfloat16 [1536, 64], replicated
- w1_shared: bfloat16 [1536, 1024], replicated
- w3_shared: bfloat16 [1536, 1024], replicated
- w2_shared: bfloat16 [1024, 1536], replicated
Outputs:
- output: bfloat16 [8192, 1536], P(('dp', 'ep'))
All inputs are finite; a program needn't handle non-finite values.
Results may differ from a plain program's by a relative error of at most 0.00656328.
Values are sent between devices in bfloat16 or wider.
A program may use at most 1 GiB of HBM per device.

v0:
```python
import jax
import jax.numpy as jnp
from jax import lax
from jax.sharding import PartitionSpec as P

ROUTE_SCALE = 2.5


def gate_weights(x_tokens, assign, slot_expert, w_router):
    logits = jnp.dot(x_tokens, w_router, preferred_element_type=jnp.float32)
    gate_prob = jax.nn.sigmoid(logits)
    is_kept = assign >= 0
    chosen = jnp.take(slot_expert, jnp.maximum(assign, 0))
    picked = jnp.where(is_kept, jnp.take_along_axis(gate_prob, chosen, axis=1), 0.0)
    gate_total = jnp.sum(picked, axis=1, keepdims=True)
    return ROUTE_SCALE * picked / jnp.maximum(gate_total, 1e-30), is_kept


def shared_expert(x_tokens, w1_shared, w3_shared, w2_shared):
    h_gate = jnp.dot(x_tokens, w1_shared, preferred_element_type=jnp.float32)
    h_up = jnp.dot(x_tokens, w3_shared, preferred_element_type=jnp.float32)
    mid_act = (jax.nn.silu(h_gate) * h_up).astype(jnp.bfloat16)
    return jnp.dot(mid_act, w2_shared, preferred_element_type=jnp.float32)


def solution(mesh):
    group_size = mesh.shape['ep']

    def device_step(x_tokens, slot_expert, w1_slots, w3_slots, w2_slots, assign, w_router, w1_shared, w3_shared, w2_shared):
        tok_dev, dim_model = x_tokens.shape
        top_k = assign.shape[1]
        local_slots = w1_slots.shape[0]
        num_slots = local_slots * group_size
        cap_rows = max(4, (3 * tok_dev * top_k) // num_slots)
        route_weight, is_kept = gate_weights(x_tokens, assign, slot_expert, w_router)
        shared_out = shared_expert(x_tokens, w1_shared, w3_shared, w2_shared)
        flat_slot = jnp.where(is_kept, assign, num_slots).reshape(-1)
        onehot = (flat_slot[:, None] == jnp.arange(num_slots, dtype=jnp.int32)[None, :]).astype(jnp.int32)
        slot_rank = jnp.sum(jnp.cumsum(onehot, axis=0) * onehot, axis=1) - 1
        dummy_row = num_slots * cap_rows
        row_pos = jnp.where(flat_slot < num_slots, flat_slot * cap_rows + slot_rank, dummy_row)
        token_ids = jnp.arange(tok_dev * top_k, dtype=jnp.int32) // top_k
        row_token = jnp.full((dummy_row + 1,), tok_dev, jnp.int32).at[row_pos].set(token_ids)[:dummy_row]
        send_rows = jnp.take(x_tokens, row_token, axis=0, mode='fill', fill_value=0)
        recv_rows = lax.all_to_all(send_rows, 'ep', 0, 0, tiled=True)
        recv_rows = recv_rows.reshape(group_size, local_slots, cap_rows, dim_model)
        h_gate = jnp.einsum('jlcd,ldf->jlcf', recv_rows, w1_slots, preferred_element_type=jnp.float32)
        h_up = jnp.einsum('jlcd,ldf->jlcf', recv_rows, w3_slots, preferred_element_type=jnp.float32)
        mid_act = (jax.nn.silu(h_gate) * h_up).astype(jnp.bfloat16)
        expert_out = jnp.einsum('jlcf,lfd->jlcd', mid_act, w2_slots, preferred_element_type=jnp.float32).astype(jnp.bfloat16)
        back_rows = lax.all_to_all(expert_out.reshape(dummy_row, dim_model), 'ep', 0, 0, tiled=True)
        gathered = jnp.take(back_rows, jnp.minimum(row_pos, dummy_row - 1), axis=0).reshape(tok_dev, top_k, dim_model)
        routed = jnp.sum(route_weight[:, :, None] * gathered, axis=1)
        return (shared_out + routed).astype(jnp.bfloat16)

    token_spec = P(('dp', 'ep'), None)
    slot_spec = P('ep', None, None)
    return jax.shard_map(device_step, mesh=mesh, in_specs=(token_spec, P(), slot_spec, slot_spec, slot_spec, token_spec, P(), P(), P(), P()), out_specs=token_spec, check_vma=False)
```

profile of v0, /device:TPU:9, one launch (start us, length us, event | category | flops | bytes accessed | tf_op | source)
XLA Modules:
  0.0 272.4 jit_solution(13497962611157836406)
XLA Ops:
  0.0 0.0 copy-start
  0.0 0.0 copy-start.2
  0.0 0.9 copy.21
  0.9 0.1 eq.26
  1.1 0.1 reshape.167
  1.2 0.1 copy.24
  1.4 0.2 fusion.26
  1.6 0.0 copy-start.4
  1.6 0.7 copy-done.4
  2.3 1.0 broadcast_add_fusion
  3.3 0.2 fusion.33
  3.6 0.1 sub.15
  3.7 0.1 lt.84
  3.9 0.1 mul.62
  4.1 2.9 %scatter_custom_fusion = s32[1153]{0:T(1024)S(1)} fusion(s32[384]{0:T(512)S(1)} %get-tuple-element.6, s32[384]{0:T(512)S(1)} %add_select_fusion, s32[]{:T(128)} %constant.63.clone.1), kind=kCustom, calls=%fused_computation.66 | custom fusion | bytes 4616 | tf_op jit(solution)/shard_map/scatter | solution.py:43
  7.0 0.0 copy-done.2
  7.0 5.4 %gather_fusion.1 = bf16[1152,1536]{1,0:T(8,128)(2,1)} fusion(bf16[64,1536]{1,0:T(8,128)(2,1)S(1)} %copy-done.2, s32[2048]{0:T(1024)S(1)} %pad_clamp_fusion), kind=kCustom, calls=%fused_computation.1 | custom fusion | bytes 7082496 | tf_op jit(solution)/shard_map/jit(_take)/gather | solution.py:44
  12.4 7.3 %gather.23 = bf16[128,9,1536]{2,1,0:T(8,128)(2,1)} reshape(bf16[1152,1536]{1,0:T(8,128)(2,1)} %gather_fusion.1) | data formatting | bytes 7077888 | tf_op jit(solution)/shard_map/jit(_take)/gather | solution.py:44
  19.6 0.2 slice.14
  19.9 3.8 %broadcast_select_fusion = bf16[128,9,1536]{2,1,0:T(8,128)(2,1)S(1)} fusion(bf16[128,9,1536]{2,1,0:T(8,128)(2,1)} %gather.23, pred[128,9]{1,0:T(8,128)(4,1)S(1)} %compare_and_fusion), kind=kLoop, calls=%fused_computation.5 | loop fusion | flops 1769472 | bytes 7079040 | tf_op jit(solution)/shard_map/jit(_take)/select_n | solution.py:44
  23.7 0.0 copy-start.5
  23.7 93.8 %all_to_all.15 = bf16[128,9,1536]{2,1,0:T(8,128)(2,1)S(1)} all-to-all(bf16[128,9,1536]{2,1,0:T(8,128)(2,1)S(1)} %broadcast_select_fusion), channel_id=1, replica_groups=mesh['dp'=1,'ep'=128] {'ep'}, dimensions={0} | all-to-all | bytes 7077888 | tf_op jit(solution)/shard_map/all_to_all | solution.py:45
  117.5 0.0 copy-start.3
  117.5 2.7 copy-done.3
  120.2 0.0 copy-done.5
  120.2 5.4 %fusion.5 = f32[128,9,512]{2,0,1:T(8,128)} fusion(bf16[128,9,1536]{2,1,0:T(8,128)(2,1)S(1)} %all_to_all.15, bf16[1,1536,512]{2,1,0:T(8,128)(2,1)S(1)} %copy-done.5), kind=kOutput, calls=%fused_computation.17 | convolution fusion | flops 1811939328 | bytes 7471104 | tf_op jit(solution)/shard_map/jlcd,ldf->jlcf/dot_general | solution.py:48
  125.6 12.2 %convolution_convert_fusion = bf16[128,9,1536]{2,0,1:T(8,128)(2,1)} fusion(bf16[1,512,1536]{2,1,0:T(8,128)(2,1)} %param.14, f32[128,9,512]{2,0,1:T(8,128)} %fusion.5, bf16[128,9,1536]{2,1,0:T(8,128)(2,1)} %copy-done.3, bf16[1,1536,512]{2,1,0:T(8,128)(2,1)} %param.12), kind=kOutput, calls=%fused_computation.6 | convolution fusion | flops 3629187072 | bytes 12582912 | tf_op jit(solution)/shard_map/jlcf,lfd->jlcd/dot_general | solution.py:50
  137.8 7.2 %copy.28 = bf16[128,9,1536]{2,1,0:T(8,128)(2,1)} copy(bf16[128,9,1536]{2,0,1:T(8,128)(2,1)} %convolution_convert_fusion) | data formatting | bytes 7077888 | tf_op jit(solution)/shard_map/convert_element_type | solution.py:50
  145.0 12.9 %all-to-all-start.1 = ((bf16[128,9,1536]{2,1,0:T(8,128)(2,1)}), bf16[128,9,1536]{2,1,0:T(8,128)(2,1)}, u32[]{:S(2)}, u32[]{:S(2)}) async-start(bf16[128,9,1536]{2,1,0:T(8,128)(2,1)} %copy.28), calls=%async_computation.1 | async-start | bytes 12582912 | tf_op jit(solution)/shard_map/all_to_all | solution.py:51
  157.9 0.0 copy-start.1
  157.9 0.1 reshape.175
  158.1 0.5 copy-done.1
  158.5 2.7 gather_fusion
  161.2 0.1 reshape.174
  161.4 0.1 reshape.197
  161.5 1.1 fusion.17
  162.7 2.9 %gather_fusion.3 = f32[384]{0:T(512)S(1)} fusion(f32[64,64]{1,0:T(8,128)S(1)} %fusion.17, s32[384]{0:T(512)S(1)} %reshape.197), kind=kCustom, calls=%fused_computation.3 | custom fusion | bytes 6144 | tf_op jit(solution)/shard_map/jit(take_along_axis)/gather | solution.py:14
  165.6 0.1 reshape.200
  165.7 0.1 fusion.45
  165.8 0.1 multiply_divide_fusion
  165.9 3.2 %fusion.47 = f32[64,1024]{1,0:T(8,128)} fusion(bf16[64,1536]{1,0:T(8,128)(2,1)S(1)} %copy-done.2, bf16[1536,1024]{1,0:T(8,128)(2,1)} %param.17), kind=kOutput, calls=%fused_computation.82 | convolution fusion | flops 201326592 | bytes 3604480 | tf_op jit(solution)/shard_map/dot_general | solution.py:20
  169.2 78.4 %all-to-all-done.1 = bf16[128,9,1536]{2,1,0:T(8,128)(2,1)} async-done(((bf16[128,9,1536]{2,1,0:T(8,128)(2,1)}), bf16[128,9,1536]{2,1,0:T(8,128)(2,1)}, u32[]{:S(2)}, u32[]{:S(2)}) %all-to-all-start.1) | async-done | bytes 3538976 | tf_op jit(solution)/shard_map/all_to_all | solution.py:51
  247.6 7.5 %all_to_all.12 = bf16[1152,1536]{1,0:T(8,128)(2,1)} reshape(bf16[128,9,1536]{2,1,0:T(8,128)(2,1)} %all-to-all-done.1) | data formatting | bytes 7077888 | tf_op jit(solution)/shard_map/all_to_all | solution.py:51
  255.0 6.7 %gather_fusion.2 = bf16[384,1536]{1,0:T(8,128)(2,1)} fusion(bf16[1152,1536]{1,0:T(8,128)(2,1)} %all_to_all.12, s32[1024]{0:T(1024)S(1)} %pad_clamp_fusion.1), kind=kCustom, calls=%fused_computation.2 | custom fusion | bytes 2360832 | tf_op jit(solution)/shard_map/jit(_take)/gather | solution.py:52
  261.8 3.0 %gather.25 = bf16[64,6,1536]{2,1,0:T(8,128)(2,1)} reshape(bf16[384,1536]{1,0:T(8,128)(2,1)} %gather_fusion.2) | data formatting | bytes 2359296 | tf_op jit(solution)/shard_map/jit(_take)/gather | solution.py:52
  264.8 3.6 %multiply_reduce_fusion = f32[64,1536]{1,0:T(8,128)} fusion(bf16[64,6,1536]{2,1,0:T(8,128)(2,1)} %gather.25, f32[64,6]{1,0:T(8,128)S(1)} %multiply_divide_fusion, pred[64,6]{1,0:T(8,128)(4,1)S(1)} %get-tuple-element.9), kind=kLoop, calls=%fused_computation.7 | loop fusion | flops 2260992 | bytes 1574784 | tf_op jit(solution)/shard_map/reduce_sum | solution.py:53
  268.4 0.0 copy-done
  268.4 3.9 %fusion.4 = bf16[64,1536]{1,0:T(8,128)(2,1)} fusion(f32[64,1536]{1,0:T(8,128)} %multiply_reduce_fusion, bf16[1024,1536]{1,0:T(8,128)(2,1)S(1)} %copy-done, bf16[64,1536]{1,0:T(8,128)(2,1)S(1)} %copy-done.2, bf16[1536,1024]{1,0:T(8,128)(2,1)} %param.18, f32[64,1024]{1,0:T(8,128)} %fusion.47), kind=kOutput, calls=%fused_computation.16 | convolution fusion | flops 403243008 | bytes 7340032 | tf_op jit(solution)/shard_map/dot_general | solution.py:23
  (15 shorter events, 0.2 us)
Async XLA Ops:
  0.0 268.4 %copy-start = (bf16[1024,1536]{1,0:T(8,128)(2,1)S(1)}, bf16[1024,1536]{1,0:T(8,128)(2,1)}, u32[]{:S(2)}) copy-start(bf16[1024,1536]{1,0:T(8,128)(2,1)} %param.19) | copy-start | bytes 9437188
  0.0 7.0 %copy-start.2 = (bf16[64,1536]{1,0:T(8,128)(2,1)S(1)}, bf16[64,1536]{1,0:T(8,128)(2,1)}, u32[]{:S(2)}) copy-start(bf16[64,1536]{1,0:T(8,128)(2,1)} %param.10) | copy-start | bytes 589828
  1.6 0.7 copy-start.4
  23.7 96.5 %copy-start.5 = (bf16[1,1536,512]{2,1,0:T(8,128)(2,1)S(1)}, bf16[1,1536,512]{2,1,0:T(8,128)(2,1)}, u32[]{:S(2)}) copy-start(bf16[1,1536,512]{2,1,0:T(8,128)(2,1)} %param.13) | copy-start | bytes 4718596
  117.5 2.7 copy-start.3
  145.0 102.6 %all-to-all-start.1 = ((bf16[128,9,1536]{2,1,0:T(8,128)(2,1)}), bf16[128,9,1536]{2,1,0:T(8,128)(2,1)}, u32[]{:S(2)}, u32[]{:S(2)}) async-start(bf16[128,9,1536]{2,1,0:T(8,128)(2,1)} %copy.28), calls=%async_computation.1 | async-start | bytes 12582912 | tf_op jit(solution)/shard_map/all_to_all | solution.py:51
  157.9 0.7 copy-start.1
where the time goes:
time: 273 us; the launch traced here: 272 us
  blocking collectives  93.8 us (34%)
  waiting for transfers between devices  78.4 us (29%)
  local copies, waits for them, and re-layouts  51.9 us (19%)
  matrix products  26 us (10%)
  starting transfers between devices  12.9 us (5%)
  other arithmetic  9.26 us (3%)
    all_to_all x1, blocking collectives, device_step(): recv_rows = lax.all_to_all(send_rows, 'ep', 0, 0, tiled=True)  93.8 us
    all_to_all x1, waiting for transfers between devices, device_step(): lax.all_to_all(expert_out.reshape(dummy_row, dim_model), 'ep', 0, 0, tile...  78.4 us
    all_to_all x1, starting transfers between devices, device_step(): lax.all_to_all(expert_out.reshape(dummy_row, dim_model), 'ep', 0, 0, tile...  12.9 us
    gather x2, local copies, waits for them, and re-layouts, device_step(): send_rows = jnp.take(x_tokens, row_token, axis=0, mode='fill', fill_value=0)  12.6 us
    dot_general x1, matrix products, device_step(): jnp.einsum('jlcf,lfd->jlcd', mid_act, w2_slots, preferred_element_type=jn...  12.2 us
    gather x2, local copies, waits for them, and re-layouts, device_step(): jnp.take(back_rows, jnp.minimum(row_pos, dummy_row - 1), axis=0)  9.75 us
    all_to_all x1, local copies, waits for them, and re-layouts, device_step(): lax.all_to_all(expert_out.reshape(dummy_row, dim_model), 'ep', 0, 0, tile...  7.49 us
    convert_element_type x1, local copies, waits for them, and re-layouts, device_step(): jnp.einsum('jlcf,lfd->jlcd', mid_act, w2_slots, preferred_element_type=jn...  7.16 us
  transfers between devices with their start and end apart: 1, of which 1 were waited for; matrix products, arithmetic and copies ran while one was open for 4% of the time, Pallas kernels for 0%

commit v1 on v0

v1 whole, which is shorter than its diff:
```python
import jax
import jax.numpy as jnp
from jax import lax
from jax.experimental import pallas as pl
from jax.experimental.pallas import tpu as pltpu
from jax.sharding import PartitionSpec as P

ROUTE_SCALE = 2.5
RING = 4
CAP = 9
BF16 = jnp.bfloat16
F32 = jnp.float32
STRIDE = {'x': 2, 'y': 8, 'z': 32}
CLASSES = (('y', 'z', 'x'), ('z', 'x', 'y'), ('x', 'y', 'z'))


def iota(shape, dim):
    return lax.broadcasted_iota(jnp.int32, shape, dim)


def dot(a, b):
    return jnp.dot(a, b, preferred_element_type=F32)


def as_onehot(cond):
    return jnp.where(cond, 1.0, 0.0).astype(BF16)


def three_parts(v):
    hi = v.astype(BF16)
    rest = v - hi.astype(F32)
    mid = rest.astype(BF16)
    lo = (rest - mid.astype(F32)).astype(BF16)
    return hi, mid, lo


def moe_kernel(x_ref, assign_ref, slot_expert_ref, wr_ref, w1_hbm, w3_hbm, w2_hbm, s1_hbm, s3_hbm, s2_hbm, y_ref,
               G, T, tab, Pm, Sb, R, Ob, Hb, Z, F, zs, w1, w3, w2, s1, s3, s2,
               wsem, lsem, g1s, g1r, g2s, g2r, t1s, t1r, t2s, t2r, d3s, d3r, d5s, d5r, d6s, d6r):
    me = lax.axis_index('ep')
    core = me % 2
    pos = {'x': (me // 2) % RING, 'y': (me // 8) % RING, 'z': me // 32}
    third = x_ref.shape[1] // 3

    def moved(axis, value):
        return (value - pos[axis]) * STRIDE[axis]

    def remote(src, dst, ssem, rsem, dev):
        return pltpu.make_async_remote_copy(src_ref=src, dst_ref=dst, send_sem=ssem, recv_sem=rsem,
                                            device_id={'ep': dev}, device_id_type=pl.DeviceIdType.MESH)

    barrier = pltpu.get_barrier_semaphore()
    partners = 0

    def greet(dev):
        pl.semaphore_signal(barrier, inc=1, device_id={'ep': dev}, device_id_type=pl.DeviceIdType.MESH)

    other = 1 - 2 * core
    greet(me + other)
    partners += 1
    for axis in 'xyz':
        for d in range(1, RING):
            dev = me + moved(axis, (pos[axis] + d) % RING)
            greet(dev)
            greet(dev + other)
            partners += 2
    for a, b, _ in CLASSES:
        for d in range(1, RING):
            for e in range(1, RING):
                greet(me + moved(a, (pos[a] + d) % RING) + moved(b, (pos[b] + e) % RING))
                partners += 1

    weight_copies = [pltpu.make_async_copy(s, d, wsem.at[i]) for i, (s, d) in enumerate(
        ((s1_hbm, s1), (s3_hbm, s3), (s2_hbm, s2), (w1_hbm.at[0], w1), (w3_hbm.at[0], w3), (w2_hbm.at[0], w2)))]
    for c in weight_copies:
        c.start()

    tokens = x_ref.shape[0]
    slots = slot_expert_ref.shape[1]
    slot_lane = iota((tokens, slots), 1)
    chosen = jnp.zeros((tokens, slots), F32)
    for k in range(assign_ref.shape[1]):
        chosen = chosen + jnp.where(assign_ref[:, k:k + 1] == slot_lane, 1.0, 0.0)
    lower = as_onehot(iota((tokens, tokens), 1) < iota((tokens, tokens), 0))
    rank = jnp.where(chosen > 0.5, dot(lower, chosen.astype(BF16)), 99.0)
    token_id = (iota((tokens, slots), 0) + 1).astype(F32)
    tab_rows = [jnp.sum(jnp.where(rank == float(r), token_id, 0.0), axis=0, keepdims=True) for r in range(CAP)]
    tab[...] = jnp.concatenate(tab_rows + [jnp.zeros((16 - CAP, slots), F32)], axis=0).astype(BF16)

    pl.semaphore_wait(barrier, partners)

    for cls, (a1, a2, a3) in enumerate(CLASSES):
        cols = pl.ds(cls * third, third)
        here = (cls, pos[a2], pos[a1])
        for d in (2, 1, 3):
            dev = me + moved(a1, (pos[a1] + d) % RING)
            remote(tab, T.at[here], t1s.at[cls, d], t1r.at[cls, d], dev).start()
            remote(x_ref.at[:, cols], G.at[here], g1s.at[cls, d], g1r.at[cls, d], dev).start()
        pltpu.make_async_copy(tab, T.at[here], t1r.at[cls, 0]).start()
        pltpu.make_async_copy(x_ref.at[:, cols], G.at[here], g1r.at[cls, 0]).start()

    gate = jax.nn.sigmoid(dot(x_ref[...], wr_ref[...]))
    num_experts = wr_ref.shape[1]
    slot_of = as_onehot(iota((num_experts, slots), 0) == slot_expert_ref[...])
    gate_slot = sum(dot(p, slot_of) for p in three_parts(gate))
    picked = jnp.where(chosen > 0.5, gate_slot, 0.0)
    route = ROUTE_SCALE * picked / jnp.maximum(jnp.sum(picked, axis=1, keepdims=True), 1e-30)
    route_parts = jnp.concatenate(three_parts(route), axis=0)
    rank_bf = rank.astype(BF16)

    for cls, (a1, a2, a3) in enumerate(CLASSES):
        cols = pl.ds(cls * third, third)
        here = (cls, pos[a2], pos[a1])
        for d in range(RING):
            pltpu.make_async_copy(tab, T.at[here], t1r.at[cls, d]).wait()
            pltpu.make_async_copy(x_ref.at[:, cols], G.at[here], g1r.at[cls, d]).wait()
        row = (cls, pos[a2])
        for d in (2, 1, 3):
            dev = me + moved(a2, (pos[a2] + d) % RING)
            remote(T.at[row], T.at[row], t2s.at[cls, d], t2r.at[cls, d], dev).start()
            remote(G.at[row], G.at[row], g2s.at[cls, d], g2r.at[cls, d], dev).start()

    for c in weight_copies[:3]:
        c.wait()
    ff_shared = s1.shape[1]
    step = 512
    acc = jnp.zeros((tokens, x_ref.shape[1]), F32)
    for f in range(0, ff_shared, step):
        xs = x_ref[...]
        mid = (jax.nn.silu(dot(xs, s1[:, f:f + step])) * dot(xs, s3[:, f:f + step])).astype(BF16)
        acc = acc + dot(mid, s2[f:f + step, :])
    zs[...] = acc

    rows = CAP * 16
    qi, qj = iota((rows, 256), 0), iota((rows, 256), 1)
    by_rank = as_onehot(qj == (qi % 16) * 16 + qi // 16)
    src_base = ((iota((rows, 128), 0) % 16) * tokens).astype(F32)
    lane = iota((rows, 128), 1).astype(F32)
    for cls, (a1, a2, a3) in enumerate(CLASSES):
        row = (cls, pos[a2])
        for d in (2, 1, 3):
            pltpu.make_async_copy(T.at[row], T.at[row], t2r.at[cls, d]).wait()
            pltpu.make_async_copy(G.at[row], G.at[row], g2r.at[cls, d]).wait()
        tabs = dot(by_rank, T[cls].reshape(256, slots)).astype(BF16)
        line = me - core - pos[a3] * STRIDE[a3]

        def select(i, _, cls=cls, a3=a3, tabs=tabs, line=line):
            d = (i + 2) % RING
            v = (pos[a3] + d) % RING
            for e in range(2):
                slot = line + v * STRIDE[a3] + (core + e) % 2
                pick = as_onehot(iota((slots, 128), 0) == slot)
                val = dot(tabs, pick)
                code = jnp.where(val > 0.5, val - 1.0 + src_base, -1.0)
                for b in range(16 * tokens // 128):
                    Pm[e * rows:(e + 1) * rows, b * 128:(b + 1) * 128] = as_onehot(code == lane + float(b * 128))
            out = dot(Pm[...], G[cls].reshape(16 * tokens, third)).astype(BF16)
            Sb[cls, pl.ds(2 * d, 2)] = out.reshape(2, CAP, 16, third)
            for e in range(2):
                k = 2 * d + e
                dev = me + moved(a3, v) + (core + e) % 2 - core
                src, dst = Sb.at[cls, k], R.at[cls, pl.ds(core * CAP, CAP), pos[a3]]
                if e == 0:
                    @pl.when(d == 0)
                    def _():
                        pltpu.make_async_copy(src, dst, d3r.at[cls, k]).start()

                    @pl.when(d != 0)
                    def _():
                        remote(src, dst, d3s.at[cls, k], d3r.at[cls, k], dev).start()
                else:
                    remote(src, dst, d3s.at[cls, k], d3r.at[cls, k], dev).start()
            return 0

        lax.fori_loop(0, RING, select, 0)

    for c in weight_copies[3:]:
        c.wait()
    blk = 3 * 64
    pi, pj = iota((blk, blk), 0), iota((blk, blk), 1)

    def bits(v):
        return v // 16 % 4, v // 4 % 4, v % 4

    ix, iz, iy = bits(pi)
    jx, jz, jy = bits(pj)
    to_first = {1: as_onehot(pj == pi // 64 * 64 + iy * 16 + ix * 4 + iz),
                2: as_onehot(pj == pi // 64 * 64 + iz * 16 + iy * 4 + ix)}
    from_first = {1: as_onehot(pi == pj // 64 * 64 + jy * 16 + jx * 4 + jz),
                  2: as_onehot(pi == pj // 64 * 64 + jz * 16 + jy * 4 + jx)}

    def permuted(mats, cls, value):
        if cls == 0:
            return value
        return jnp.concatenate([dot(mats[cls], value[i:i + blk]).astype(BF16)
                                for i in range(0, value.shape[0], blk)], axis=0)

    def expert(e, _):
        half = (core + e) % 2
        for cls in range(3):
            for d in range(RING):
                pltpu.make_async_copy(Sb.at[cls, 0], Sb.at[cls, 0], d3r.at[cls, 2 * d + e]).wait()
        n = CAP * 64
        xs = jnp.concatenate([permuted(to_first, cls, R[cls, pl.ds(half * CAP, CAP)].reshape(n, third))
                              for cls in range(3)], axis=1)
        mid = (jax.nn.silu(dot(xs, w1[...])) * dot(xs, w3[...])).astype(BF16)
        for cls, (a1, a2, a3) in enumerate(CLASSES):
            out = dot(mid, w2[:, cls * third:(cls + 1) * third]).astype(BF16)
            Ob[cls, pl.ds(half * CAP, CAP)] = permuted(from_first, cls, out).reshape(CAP, RING, 16, third)
            for d in (2, 1, 3, 0):
                v = (pos[a3] + d) % RING
                k = 2 * d + e
                dev = me + moved(a3, v) + half - core
                src, dst = Ob.at[cls, pl.ds(half * CAP, CAP), v], Hb.at[cls, :, pos[a3] * 2 + core]
                if d == 0:
                    @pl.when(e == 0)
                    def _():
                        pltpu.make_async_copy(src, dst, d5r.at[cls, k]).start()

                    @pl.when(e != 0)
                    def _():
                        remote(src, dst, d5s.at[cls, k], d5r.at[cls, k], dev).start()
                else:
                    remote(src, dst, d5s.at[cls, k], d5r.at[cls, k], dev).start()
        return 0

    lax.fori_loop(0, 2, expert, 0)

    ri, rj = iota((256, 256), 0), iota((256, 256), 1)
    by_source = as_onehot(rj == ri // 8 % 2 * 128 + ri % 8 * 16 + ri // 16)
    for cls, (a1, a2, a3) in enumerate(CLASSES):
        for k in range(8):
            pltpu.make_async_copy(Hb.at[cls, :, 0], Hb.at[cls, :, 0], d5r.at[cls, k]).wait()
        for rp in range(5):
            if rp < 4:
                out = dot(by_source, Hb[cls, 2 * rp:2 * rp + 2].reshape(256, third))
            else:
                out = dot(by_source[:, :128], Hb[cls, 8].reshape(128, third))
            Z[cls, rp] = out.astype(BF16).reshape(16, 16, third)

        home = pos[a2] * RING + pos[a1]

        def send_home(k, _, cls=cls, a1=a1, a2=a2, home=home):
            v2, v1 = (pos[a2] + k // RING) % RING, (pos[a1] + k % RING) % RING
            dev = me + moved(a2, v2) + moved(a1, v1)
            remote(Z.at[cls, :, v2 * RING + v1], F.at[cls, :, home], d6s.at[cls, k], d6r.at[cls, k], dev).start()
            return 0

        lax.fori_loop(1, 16, send_home, 0)
        pltpu.make_async_copy(Z.at[cls, :, home], F.at[cls, :, home], d6r.at[cls, 0]).start()

    ei, ej = iota((slots, 256), 0), iota((slots, 256), 1)
    rank_bit = (iota((tokens, 256), 1) // 8 % 2).astype(F32)
    for cls, (a1, a2, a3) in enumerate(CLASSES):
        slot = ej // 64 * STRIDE[a2] + ej // 16 % 4 * STRIDE[a1] + ej // 2 % 4 * STRIDE[a3] + ej % 2
        spread = as_onehot(ei == slot)
        rank_exp = dot(rank_bf, spread) - rank_bit
        w_exp = dot(route_parts, spread)
        for k in range(16):
            pltpu.make_async_copy(Z.at[cls, :, 0], Z.at[cls, :, 0], d6r.at[cls, k]).wait()
        acc = jnp.zeros((3 * tokens, third), F32)
        for rp in range(5):
            hit = rank_exp == float(2 * rp)
            w = jnp.where(jnp.concatenate([hit, hit, hit], axis=0), w_exp, 0.0).astype(BF16)
            acc = acc + dot(w, F[cls, rp].reshape(256, third))
        routed = acc[2 * tokens:] + acc[tokens:2 * tokens] + acc[:tokens]
        y_ref[:, cls * third:(cls + 1) * third] = (zs[:, cls * third:(cls + 1) * third] + routed).astype(BF16)

    for cls, (a1, a2, a3) in enumerate(CLASSES):
        here = (cls, pos[a2], pos[a1])
        row = (cls, pos[a2])
        for d in range(1, RING):
            pltpu.make_async_copy(tab, T.at[here], t1s.at[cls, d]).wait()
            pltpu.make_async_copy(x_ref.at[:, pl.ds(cls * third, third)], G.at[here], g1s.at[cls, d]).wait()
            pltpu.make_async_copy(T.at[row], T.at[row], t2s.at[cls, d]).wait()
            pltpu.make_async_copy(G.at[row], G.at[row], g2s.at[cls, d]).wait()
        for k in range(1, 8):
            pltpu.make_async_copy(Sb.at[cls, 0], Sb.at[cls, 0], d3s.at[cls, k]).wait()
            pltpu.make_async_copy(Sb.at[cls, 0], Sb.at[cls, 0], d5s.at[cls, k]).wait()
        for k in range(1, 16):
            pltpu.make_async_copy(Z.at[cls, :, 0], Z.at[cls, :, 0], d6s.at[cls, k]).wait()


def solution(mesh):
    def device_step(x_tokens, slot_expert, w1_slots, w3_slots, w2_slots, assign, w_router, w1_shared, w3_shared, w2_shared):
        tokens, dim = x_tokens.shape
        third = dim // 3
        vmem = pl.BlockSpec(memory_space=pltpu.VMEM)
        hbm = pl.BlockSpec(memory_space=pl.ANY)
        dma = pltpu.SemaphoreType.DMA
        V = pltpu.VMEM
        return pl.pallas_call(
            moe_kernel,
            out_shape=jax.ShapeDtypeStruct((tokens, dim), BF16),
            in_specs=[vmem] * 4 + [hbm] * 6,
            out_specs=vmem,
            scratch_shapes=[
                V((3, RING, RING, tokens, third), BF16),
                V((3, RING, RING, 16, slot_expert.shape[0]), BF16),
                V((16, slot_expert.shape[0]), BF16),
                V((2 * CAP * 16, 16 * tokens), BF16),
                V((3, 8, CAP, 16, third), BF16),
                V((3, 2 * CAP, RING, 16, third), BF16),
                V((3, 2 * CAP, RING, 16, third), BF16),
                V((3, CAP, 8, 16, third), BF16),
                V((3, 5, 16, 16, third), BF16),
                V((3, 5, 16, 16, third), BF16),
                V((tokens, dim), F32),
                V(w1_slots.shape[1:], BF16), V(w3_slots.shape[1:], BF16), V(w2_slots.shape[1:], BF16),
                V(w1_shared.shape, BF16), V(w3_shared.shape, BF16), V(w2_shared.shape, BF16),
                dma((6,)), dma((3,)),
                dma((3, 4)), dma((3, 4)), dma((3, 4)), dma((3, 4)),
                dma((3, 4)), dma((3, 4)), dma((3, 4)), dma((3, 4)),
                dma((3, 8)), dma((3, 8)), dma((3, 8)), dma((3, 8)),
                dma((3, 16)), dma((3, 16)),
            ],
            compiler_params=pltpu.CompilerParams(collective_id=0, has_side_effects=True,
                                                 vmem_limit_bytes=60 * 2 ** 20),
        )(x_tokens, assign, slot_expert.reshape(1, -1), w_router, w1_slots, w3_slots, w2_slots,
          w1_shared, w3_shared, w2_shared)

    token_spec = P(('dp', 'ep'), None)
    slot_spec = P('ep', None, None)
    return jax.shard_map(device_step, mesh=mesh,
                         in_specs=(token_spec, P(), slot_spec, slot_spec, slot_spec, token_spec, P(), P(), P(), P()),
                         out_specs=token_spec, check_vma=False)
```

time: 273 us -> 121 us (0.44)
  the two profiles are of different devices: /device:TPU:9 before, /device:TPU:17 now
where the time goes in v1:
time: 121 us
  Pallas kernels  116 us (96%)
  local copies, waits for them, and re-layouts  4.84 us (4%)
    pallas_call x1, Pallas kernels, device_step(): pl.pallas_call(moe_kernel, out_shape=jax.ShapeDtypeStruct((tokens, dim),...  116 us
    unnamed x3, local copies, waits for them, and re-layouts  4.84 us

profile of v1, /device:TPU:17, one launch (start us, length us, event | category | flops | bytes accessed | tf_op | source)
XLA Modules:
  0.0 121.0 jit_solution(4807960055428126785)
XLA Ops:
  0.0 1.4 %copy.11.assign_ref = s32[64,6]{1,0:T(8,128)} copy(s32[64,6]{0,1:T(8,128)} %param.15) | data formatting | bytes 3072 | tf_op args[5]
  1.4 1.8 %copy.12.wr_ref = bf16[1536,64]{1,0:T(8,128)(2,1)} copy(bf16[1536,64]{0,1:T(8,128)(2,1)} %param.16) | data formatting | bytes 393216 | tf_op args[6]
  3.2 116.1 %shard_map.100 = bf16[64,1536]{1,0:T(8,128)(2,1)} custom-call(bf16[64,1536]{1,0:T(8,128)(2,1)} %x_ref.1, s32[64,6]{1,0:T(8,128)} %copy.11.assign_ref, s32[1,128]{1,0:T(1,128)} %bitcast.1, bf16[1536,64]{1,0:T(8,128)(2,1)} %copy.12.wr_ref, bf16[1,1536,512]{2,1,0:T(8,128)(2,1)} %w1_hbm.1, bf16[1,1536,512]{2,1,0:T(8,128)(2,1)} %w3_hbm.1, ...), custom_call_target="tpu_custom_call" | custom-call | tf_op jit(solution)/shard_map/pallas_call | solution.py:292
  119.4 1.6 %copy.14 = bf16[64,1536]{1,0:T(8,128)(2,1)} copy(bf16[64,1536]{1,0:T(8,128)(2,1)} %shard_map.100) | data formatting | bytes 393216

commit v2 on v1

v2 whole, which is shorter than its diff:
```python
import jax
import jax.numpy as jnp
from jax import lax
from jax.experimental import pallas as pl
from jax.experimental.pallas import tpu as pltpu
from jax.sharding import PartitionSpec as P

ROUTE_SCALE = 2.5
RING = 4
CAP = 9
BF16 = jnp.bfloat16
F32 = jnp.float32
STRIDE = {'x': 2, 'y': 8, 'z': 32}
CLASSES = (('y', 'z', 'x'), ('z', 'x', 'y'), ('x', 'y', 'z'))


def iota(shape, dim):
    return lax.broadcasted_iota(jnp.int32, shape, dim)


def dot(a, b):
    return jnp.dot(a, b, preferred_element_type=F32)


def dot_t(a, b):
    return lax.dot_general(a, b, (((1,), (1,)), ((), ())), preferred_element_type=F32)


def as_onehot(cond):
    return jnp.where(cond, 1.0, 0.0).astype(BF16)


def three_parts(v):
    hi = v.astype(BF16)
    rest = v - hi.astype(F32)
    mid = rest.astype(BF16)
    lo = (rest - mid.astype(F32)).astype(BF16)
    return hi, mid, lo


def moe_kernel(x_ref, assign_ref, slot_expert_ref, wr_ref, w1_hbm, w3_hbm, w2_hbm, s1_hbm, s3_hbm, s2_hbm, y_ref,
               G, T, tab, Pm, Sb, R, Ob, Hb, Z, F, Cs, Cr, U, A, zs, w1, w3, w2, s1, s3, s2,
               wsem, g1s, g1r, g2s, g2r, t1s, t1r, t2s, t2r, cs, cr, d3s, d3r, d5s, d5r, d6s, d6r, d7s, d7r):
    me = lax.axis_index('ep')
    core = me % 2
    pos = {'x': (me // 2) % RING, 'y': (me // 8) % RING, 'z': me // 32}
    third = x_ref.shape[1] // 3

    def moved(axis, value):
        return (value - pos[axis]) * STRIDE[axis]

    def step_to(axis, d):
        return (pos[axis] + d) % RING

    def remote(src, dst, ssem, rsem, dev):
        return pltpu.make_async_remote_copy(src_ref=src, dst_ref=dst, send_sem=ssem, recv_sem=rsem,
                                            device_id={'ep': dev}, device_id_type=pl.DeviceIdType.MESH)

    def local(src, dst, sem):
        return pltpu.make_async_copy(src, dst, sem)

    barrier = pltpu.get_barrier_semaphore()

    def greet(dev):
        pl.semaphore_signal(barrier, inc=1, device_id={'ep': dev}, device_id_type=pl.DeviceIdType.MESH)

    other = 1 - 2 * core
    greet(me + other)
    for axis in 'xyz':
        for d in range(1, RING):
            dev = me + moved(axis, step_to(axis, d))
            greet(dev)
            greet(dev + other)

    weight_copies = [pltpu.make_async_copy(s, d, wsem.at[i]) for i, (s, d) in enumerate(
        ((s1_hbm, s1), (s3_hbm, s3), (s2_hbm, s2), (w1_hbm.at[0], w1), (w3_hbm.at[0], w3), (w2_hbm.at[0], w2)))]
    for c in weight_copies:
        c.start()

    tokens = x_ref.shape[0]
    slots = slot_expert_ref.shape[1]
    slot_row = iota((slots, tokens), 0)
    chosen_t = jnp.zeros((slots, tokens), F32)
    for k in range(assign_ref.shape[0]):
        chosen_t = chosen_t + jnp.where(assign_ref[k:k + 1, :] == slot_row, 1.0, 0.0)
    ti, tj = iota((tokens, tokens), 0), iota((tokens, tokens), 1)
    chosen = dot_t(as_onehot(ti == tj), chosen_t.astype(BF16))
    rank = jnp.where(chosen > 0.5, dot(as_onehot(tj < ti), chosen.astype(BF16)), 99.0)
    token_id = (iota((tokens, slots), 0) + 1).astype(F32)
    tab_rows = [jnp.sum(jnp.where(rank == float(r), token_id, 0.0), axis=0, keepdims=True) for r in range(CAP)]
    tab[...] = jnp.concatenate(tab_rows + [jnp.zeros((16 - CAP, slots), F32)], axis=0).astype(BF16)

    pl.semaphore_wait(barrier, 19)

    def spread(cls, k, src_t, src_g, to):
        a1, a2, _ = CLASSES[cls]
        here = (cls, pos[a2], to)
        for d in (1, 3, 2):
            dev = me + moved(a2, step_to(a2, d))
            remote(src_t, T.at[here], t2s.at[cls, k, d], t2r.at[cls, k, d], dev).start()
            remote(src_g, G.at[here], g2s.at[cls, k, d], g2r.at[cls, k, d], dev).start()

    def cols(cls):
        return x_ref.at[:, pl.ds(cls * third, third)]

    for cls, (a1, a2, a3) in enumerate(CLASSES):
        here = (cls, pos[a2], pos[a1])
        for d in (1, 3, 2):
            dev = me + moved(a1, step_to(a1, d))
            remote(tab, T.at[here], t1s.at[cls, d], t1r.at[cls, d], dev).start()
            remote(cols(cls), G.at[here], g1s.at[cls, d], g1r.at[cls, d], dev).start()
    for cls, (a1, a2, a3) in enumerate(CLASSES):
        here = (cls, pos[a2], pos[a1])
        spread(cls, 0, tab, cols(cls), pos[a1])
        local(tab, T.at[here], t1r.at[cls, 0]).start()
        local(cols(cls), G.at[here], g1r.at[cls, 0]).start()

    gate = jax.nn.sigmoid(dot_t(x_ref[...], wr_ref[...]))
    num_experts = wr_ref.shape[0]
    slot_of = as_onehot(iota((num_experts, slots), 0) == slot_expert_ref[...])
    gate_slot = sum(dot(p, slot_of) for p in three_parts(gate))
    picked = jnp.where(chosen > 0.5, gate_slot, 0.0)
    route = ROUTE_SCALE * picked / jnp.maximum(jnp.sum(picked, axis=1, keepdims=True), 1e-30)
    route_rank = jnp.concatenate(three_parts(route) + (rank.astype(BF16),), axis=1)

    for d in (3, 1, 2):
        for cls, (a1, a2, a3) in enumerate(CLASSES):
            owner = (pos[a1] + RING - d) % RING
            here = (cls, pos[a2], owner)
            local(tab, T.at[here], t1r.at[cls, d]).wait()
            local(cols(cls), G.at[here], g1r.at[cls, d]).wait()
            spread(cls, d, T.at[here], G.at[here], owner)

    si, sj = iota((4 * slots, 128), 0), iota((4 * slots, 128), 1)
    for cls, (a1, a2, a3) in enumerate(CLASSES):
        q_slot = (sj // 32 * slots + sj // 8 % 4 * STRIDE[a2] + sj // 4 % 2 + sj % 4 * STRIDE[a3])
        for v in range(RING):
            Cs[cls, v] = dot(route_rank, as_onehot(si == q_slot + v * STRIDE[a1])).astype(BF16)
        for d in (1, 3, 2, 0):
            v = step_to(a1, d)
            if d == 0:
                local(Cs.at[cls, v], Cr.at[cls, pos[a1]], cr.at[cls, d]).start()
            else:
                remote(Cs.at[cls, v], Cr.at[cls, pos[a1]], cs.at[cls, d], cr.at[cls, d], me + moved(a1, v)).start()

    for c in weight_copies[:3]:
        c.wait()
    ff_shared = s1.shape[1]
    step = 512
    acc = jnp.zeros((tokens, x_ref.shape[1]), F32)
    for f in range(0, ff_shared, step):
        xs = x_ref[...]
        mid = (jax.nn.silu(dot(xs, s1[:, f:f + step])) * dot(xs, s3[:, f:f + step])).astype(BF16)
        acc = acc + dot(mid, s2[f:f + step, :])
    zs[...] = acc

    rows = CAP * 8
    qi, qj = iota((rows, 256), 0), iota((rows, 256), 1)
    by_rank = [as_onehot(qj == (qi % 8 + 8 * h) * 16 + qi // 8) for h in range(2)]
    src_base = ((iota((rows, 128), 0) % 8) * tokens).astype(F32)
    lane = iota((rows, 128), 1).astype(F32)
    tabs, lines = [], []
    for cls, (a1, a2, a3) in enumerate(CLASSES):
        for k in range(RING):
            here = (cls, pos[a2], pos[a1])
            for d in (1, 3, 2):
                local(tab, T.at[here], t2r.at[cls, k, d]).wait()
                local(cols(cls), G.at[here], g2r.at[cls, k, d]).wait()
        local(tab, T.at[here], t1r.at[cls, 0]).wait()
        local(cols(cls), G.at[here], g1r.at[cls, 0]).wait()
        tabs.append([dot(m, T[cls].reshape(256, slots)).astype(BF16) for m in by_rank])
        lines.append(me - core - pos[a3] * STRIDE[a3])

    def select(i, _):
        e, p = i // 2, i % 2
        for cls, (a1, a2, a3) in enumerate(CLASSES):
            picks = []
            for q in range(2):
                d = 2 + q - p * (1 + 2 * q)
                slot = lines[cls] + step_to(a3, d) * STRIDE[a3] + (core + e) % 2
                picks.append(as_onehot(iota((slots, 128), 0) == slot))
            outs = []
            for h in range(2):
                for q in range(2):
                    val = dot(tabs[cls][h], picks[q])
                    code = jnp.where(val > 0.5, val - 1.0 + src_base, -1.0)
                    for b in range(8 * tokens // 128):
                        Pm[cls, h, q * rows:(q + 1) * rows, b * 128:(b + 1) * 128] = (
                            jnp.where(code == lane + float(b * 128), 1.0, 0.0))
                out = dot(Pm[cls, h].astype(BF16), G[cls, 2 * h:2 * h + 2].reshape(8 * tokens, third))
                outs.append(out.reshape(2, CAP, 8, third))
            both = jnp.concatenate(outs, axis=2).astype(BF16)
            for q in range(2):
                d = 2 + q - p * (1 + 2 * q)
                k = 2 * d + e
                Sb[cls, k] = both[q]
                dev = me + moved(a3, step_to(a3, d)) + (core + e) % 2 - core
                src, dst = Sb.at[cls, k], R.at[cls, pl.ds(core * CAP, CAP), pos[a3]]
                if q == 1:
                    @pl.when(i == 1)
                    def _():
                        local(src, dst, d3r.at[cls, k]).start()

                    @pl.when(i != 1)
                    def _():
                        remote(src, dst, d3s.at[cls, k], d3r.at[cls, k], dev).start()
                else:
                    remote(src, dst, d3s.at[cls, k], d3r.at[cls, k], dev).start()
        return 0

    lax.fori_loop(0, RING, select, 0)

    for c in weight_copies[3:]:
        c.wait()
    blk = 3 * 64
    pi, pj = iota((blk, blk), 0), iota((blk, blk), 1)

    def bits(v):
        return v // 16 % 4, v // 4 % 4, v % 4

    ix, iz, iy = bits(pi)
    jx, jz, jy = bits(pj)
    to_first = {1: as_onehot(pj == pi // 64 * 64 + iy * 16 + ix * 4 + iz),
                2: as_onehot(pj == pi // 64 * 64 + iz * 16 + iy * 4 + ix)}
    from_first = {1: as_onehot(pi == pj // 64 * 64 + jy * 16 + jx * 4 + jz),
                  2: as_onehot(pi == pj // 64 * 64 + jz * 16 + jy * 4 + jx)}

    def permuted(mats, cls, value):
        if cls == 0:
            return value
        return jnp.concatenate([dot(mats[cls], value[i:i + blk]).astype(BF16)
                                for i in range(0, value.shape[0], blk)], axis=0)

    def expert(e, _):
        half = (core + e) % 2
        for cls in range(3):
            for d in range(RING):
                local(Sb.at[cls, 0], Sb.at[cls, 0], d3r.at[cls, 2 * d + e]).wait()
        n = CAP * 64
        xs = jnp.concatenate([permuted(to_first, cls, R[cls, pl.ds(half * CAP, CAP)].reshape(n, third))
                              for cls in range(3)], axis=1)
        mid = (jax.nn.silu(dot(xs, w1[...])) * dot(xs, w3[...])).astype(BF16)
        for cls, (a1, a2, a3) in enumerate(CLASSES):
            out = dot(mid, w2[:, cls * third:(cls + 1) * third]).astype(BF16)
            Ob[cls, pl.ds(half * CAP, CAP)] = permuted(from_first, cls, out).reshape(CAP, RING, 16, third)
            for d in (2, 1, 3, 0):
                v = step_to(a3, d)
                k = 2 * d + e
                dev = me + moved(a3, v) + half - core
                src, dst = Ob.at[cls, pl.ds(half * CAP, CAP), v], Hb.at[cls, core, :, pos[a3]]
                if d == 0:
                    @pl.when(e == 0)
                    def _():
                        local(src, dst, d5r.at[cls, k]).start()

                    @pl.when(e != 0)
                    def _():
                        remote(src, dst, d5s.at[cls, k], d5r.at[cls, k], dev).start()
                else:
                    remote(src, dst, d5s.at[cls, k], d5r.at[cls, k], dev).start()
        return 0

    lax.fori_loop(0, 2, expert, 0)

    u2, v3 = pi // 16 % 4, pi // 4 % 4
    by_second = as_onehot(pj == pi // 64 * 64 + v3 * 16 + u2 * 4 + pi % 4)

    def regroup(e, _):
        half = (core + e) % 2
        for cls, (a1, a2, a3) in enumerate(CLASSES):
            for d in range(RING):
                local(Sb.at[cls, 0], Sb.at[cls, 0], d5r.at[cls, 2 * d + e]).wait()
            rows_in = Hb[cls, half].reshape(CAP * 64, third)
            Z[cls, half] = jnp.concatenate([dot(by_second, rows_in[i:i + blk]).astype(BF16) for i in
                                            range(0, CAP * 64, blk)], axis=0).reshape(CAP, RING, 16, third)
            for d in (2, 1, 3, 0):
                v = step_to(a2, d)
                src, dst = Z.at[cls, half, :, v], F.at[cls, :, pos[a2], half]
                if d == 0:
                    local(src, dst, d6r.at[cls, e, d]).start()
                else:
                    remote(src, dst, d6s.at[cls, e, d], d6r.at[cls, e, d], me + moved(a2, v)).start()
        return 0

    lax.fori_loop(0, 2, regroup, 0)

    all_tok = RING * tokens
    ei, ej = iota((128, 128), 0), iota((128, 128), 1)
    spreads = [as_onehot(ei == ej // 4 + 32 * part) for part in range(4)]
    same = iota((all_tok, 128), 0) // tokens == iota((all_tok, 128), 1) % 4
    for cls, (a1, a2, a3) in enumerate(CLASSES):
        for d in range(RING):
            local(Cs.at[cls, 0], Cr.at[cls, 0], cr.at[cls, d]).wait()
        c_all = Cr[cls].reshape(all_tok, 128)
        w_exp = [dot(c_all, spreads[part]) for part in range(3)]
        rank_exp = jnp.where(same, dot(c_all, spreads[3]), 99.0)
        for e in range(2):
            for d in range(RING):
                local(Sb.at[cls, 0], Sb.at[cls, 0], d6r.at[cls, e, d]).wait()
        acc = jnp.zeros((3 * all_tok, third), F32)
        for r0 in range(0, CAP, 2):
            ranks = range(r0, min(r0 + 2, CAP))
            w = jnp.concatenate([jnp.concatenate([jnp.where(rank_exp == float(r), w_exp[part], 0.0) for r in ranks], axis=1)
                                 for part in range(3)], axis=0).astype(BF16)
            acc = acc + dot(w, F[cls, r0:r0 + len(ranks)].reshape(128 * len(ranks), third))
        U[cls] = (acc[2 * all_tok:] + acc[all_tok:2 * all_tok] + acc[:all_tok]).reshape(RING, tokens, third)
        for d in (2, 1, 3, 0):
            v = step_to(a1, d)
            if d == 0:
                local(U.at[cls, v], A.at[cls, pos[a1]], d7r.at[cls, d]).start()
            else:
                remote(U.at[cls, v], A.at[cls, pos[a1]], d7s.at[cls, d], d7r.at[cls, d], me + moved(a1, v)).start()
    for cls in range(3):
        for d in range(RING):
            local(U.at[cls, 0], A.at[cls, 0], d7r.at[cls, d]).wait()
        routed = (A[cls, 0] + A[cls, 1]) + (A[cls, 2] + A[cls, 3])
        y_ref[:, cls * third:(cls + 1) * third] = (zs[:, cls * third:(cls + 1) * third] + routed).astype(BF16)

    for cls, (a1, a2, a3) in enumerate(CLASSES):
        here = (cls, pos[a2], pos[a1])
        for d in range(1, RING):
            local(tab, T.at[here], t1s.at[cls, d]).wait()
            local(cols(cls), G.at[here], g1s.at[cls, d]).wait()
            local(Cs.at[cls, 0], Cr.at[cls, 0], cs.at[cls, d]).wait()
            for k in range(RING):
                local(tab, T.at[here], t2s.at[cls, k, d]).wait()
                local(cols(cls), G.at[here], g2s.at[cls, k, d]).wait()
        for k in range(1, 8):
            local(Sb.at[cls, 0], Sb.at[cls, 0], d3s.at[cls, k]).wait()
            local(Sb.at[cls, 0], Sb.at[cls, 0], d5s.at[cls, k]).wait()
        for d in range(1, RING):
            local(U.at[cls, 0], A.at[cls, 0], d7s.at[cls, d]).wait()
            for e in range(2):
                local(Sb.at[cls, 0], Sb.at[cls, 0], d6s.at[cls, e, d]).wait()


def solution(mesh):
    def device_step(x_tokens, slot_expert, w1_slots, w3_slots, w2_slots, assign, w_router, w1_shared, w3_shared, w2_shared):
        tokens, dim = x_tokens.shape
        third = dim // 3
        slots = slot_expert.shape[0]
        vmem = pl.BlockSpec(memory_space=pltpu.VMEM)
        hbm = pl.BlockSpec(memory_space=pl.ANY)
        dma = pltpu.SemaphoreType.DMA
        V = pltpu.VMEM
        return pl.pallas_call(
            moe_kernel,
            out_shape=jax.ShapeDtypeStruct((tokens, dim), BF16),
            in_specs=[vmem] * 4 + [hbm] * 6,
            out_specs=vmem,
            scratch_shapes=[
                V((3, RING, RING, tokens, third), BF16),
                V((3, RING, RING, 16, slots), BF16),
                V((16, slots), BF16),
                V((3, 2, 2 * CAP * 8, 8 * tokens), F32),
                V((3, 8, CAP, 16, third), BF16),
                V((3, 2 * CAP, RING, 16, third), BF16),
                V((3, 2 * CAP, RING, 16, third), BF16),
                V((3, 2, CAP, RING, 16, third), BF16),
                V((3, 2, CAP, RING, 16, third), BF16),
                V((3, CAP, RING, 2, 16, third), BF16),
                V((3, RING, tokens, 128), BF16), V((3, RING, tokens, 128), BF16),
                V((3, RING, tokens, third), F32), V((3, RING, tokens, third), F32),
                V((tokens, dim), F32),
                V(w1_slots.shape[1:], BF16), V(w3_slots.shape[1:], BF16), V(w2_slots.shape[1:], BF16),
                V(w1_shared.shape, BF16), V(w3_shared.shape, BF16), V(w2_shared.shape, BF16),
                dma((6,)),
                dma((3, 4)), dma((3, 4)), dma((3, 4, 4)), dma((3, 4, 4)),
                dma((3, 4)), dma((3, 4)), dma((3, 4, 4)), dma((3, 4, 4)),
                dma((3, 4)), dma((3, 4)),
                dma((3, 8)), dma((3, 8)), dma((3, 8)), dma((3, 8)),
                dma((3, 2, 4)), dma((3, 2, 4)), dma((3, 4)), dma((3, 4)),
            ],
            compiler_params=pltpu.CompilerParams(collective_id=0, has_side_effects=True,
                                                 vmem_limit_bytes=60 * 2 ** 20),
        )(x_tokens, assign.T, slot_expert.reshape(1, -1), w_router.T, w1_slots, w3_slots, w2_slots,
          w1_shared, w3_shared, w2_shared)

    token_spec = P(('dp', 'ep'), None)
    slot_spec = P('ep', None, None)
    return jax.shard_map(device_step, mesh=mesh,
                         in_specs=(token_spec, P(), slot_spec, slot_spec, slot_spec, token_spec, P(), P(), P(), P()),
                         out_specs=token_spec, check_vma=False)
```

time: 121 us -> 88.7 us (0.73)
  the two profiles are of different devices: /device:TPU:17 before, /device:TPU:1 now
where the time goes in v2:
time: 88.7 us; the launch traced here: 88.5 us
  Pallas kernels  86.9 us (98%)
  local copies, waits for them, and re-layouts  1.62 us (2%)
    pallas_call x1, Pallas kernels, device_step(): pl.pallas_call(moe_kernel, out_shape=jax.ShapeDtypeStruct((tokens, dim),...  86.9 us

profile of v2, /device:TPU:1, one launch (start us, length us, event | category | flops | bytes accessed | tf_op | source)
XLA Modules:
  0.0 88.5 jit_solution(3473981257917988356)
XLA Ops:
  0.0 86.9 %shard_map.100 = bf16[64,1536]{1,0:T(8,128)(2,1)} custom-call(bf16[64,1536]{1,0:T(8,128)(2,1)} %x_ref.1, s32[6,64]{1,0:T(8,128)} %bitcast.4, s32[1,128]{1,0:T(1,128)} %bitcast.5, bf16[64,1536]{1,0:T(8,128)(2,1)} %bitcast.3, bf16[1,1536,512]{2,1,0:T(8,128)(2,1)} %w1_hbm.1, bf16[1,1536,512]{2,1,0:T(8,128)(2,1)} %w3_hbm.1, bf16[1,512,1536]{2,1,0:T(8,128)(2,1)} %w2_hbm.1, ...), custom_call_target="tpu_custom_call" | custom-call | tf_op jit(solution)/shard_map/pallas_call | solution.py:346
  86.9 1.6 %copy.12 = bf16[64,1536]{1,0:T(8,128)(2,1)} copy(bf16[64,1536]{1,0:T(8,128)(2,1)} %shard_map.100) | data formatting | bytes 393216

commit v3 on v2

--- a/solution.py
+++ b/solution.py
@@ -38,13 +38,15 @@
     return hi, mid, lo
 
 
-def moe_kernel(x_ref, assign_ref, slot_expert_ref, wr_ref, w1_hbm, w3_hbm, w2_hbm, s1_hbm, s3_hbm, s2_hbm, y_ref,
+def moe_kernel(x_hbm, assign_hbm, slot_expert_hbm, wr_hbm, w1_hbm, w3_hbm, w2_hbm, s1_hbm, s3_hbm, s2_hbm, y_ref,
+               x_ref, assign_ref, slot_expert_ref, wr_ref,
                G, T, tab, Pm, Sb, R, Ob, Hb, Z, F, Cs, Cr, U, A, zs, w1, w3, w2, s1, s3, s2,
-               wsem, g1s, g1r, g2s, g2r, t1s, t1r, t2s, t2r, cs, cr, d3s, d3r, d5s, d5r, d6s, d6r, d7s, d7r):
+               wsem, isem, g1s, g1r, g2s, g2r, t1s, t1r, t2s, t2r, cs, cr, d3s, d3r, d5s, d5r, d6s, d6r, d7s, d7r):
     me = lax.axis_index('ep')
     core = me % 2
     pos = {'x': (me // 2) % RING, 'y': (me // 8) % RING, 'z': me // 32}
     third = x_ref.shape[1] // 3
+    sixth = third // 2
 
     def moved(axis, value):
         return (value - pos[axis]) * STRIDE[axis]
@@ -72,11 +74,16 @@
             greet(dev)
             greet(dev + other)
 
+    input_copies = [local(s, d, isem.at[i]) for i, (s, d) in enumerate(
+        ((assign_hbm, assign_ref), (x_hbm, x_ref), (slot_expert_hbm, slot_expert_ref), (wr_hbm, wr_ref)))]
+    for c in input_copies:
+        c.start()
     weight_copies = [pltpu.make_async_copy(s, d, wsem.at[i]) for i, (s, d) in enumerate(
         ((s1_hbm, s1), (s3_hbm, s3), (s2_hbm, s2), (w1_hbm.at[0], w1), (w3_hbm.at[0], w3), (w2_hbm.at[0], w2)))]
     for c in weight_copies:
         c.start()
 
+    input_copies[0].wait()
     tokens = x_ref.shape[0]
     slots = slot_expert_ref.shape[1]
     slot_row = iota((slots, tokens), 0)
@@ -90,30 +97,31 @@
     tab_rows = [jnp.sum(jnp.where(rank == float(r), token_id, 0.0), axis=0, keepdims=True) for r in range(CAP)]
     tab[...] = jnp.concatenate(tab_rows + [jnp.zeros((16 - CAP, slots), F32)], axis=0).astype(BF16)
 
+    for c in input_copies[1:]:
+        c.wait()
     pl.semaphore_wait(barrier, 19)
 
-    def spread(cls, k, src_t, src_g, to):
-        a1, a2, _ = CLASSES[cls]
-        here = (cls, pos[a2], to)
+    def cols(cls, g):
+        return x_ref.at[:, pl.ds((2 * cls + g) * sixth, sixth)]
+
+    def spread(cls, g, k, src, to):
+        a2 = CLASSES[cls][1]
         for d in (1, 3, 2):
-            dev = me + moved(a2, step_to(a2, d))
-            remote(src_t, T.at[here], t2s.at[cls, k, d], t2r.at[cls, k, d], dev).start()
-            remote(src_g, G.at[here], g2s.at[cls, k, d], g2r.at[cls, k, d], dev).start()
-
-    def cols(cls):
-        return x_ref.at[:, pl.ds(cls * third, third)]
-
-    for cls, (a1, a2, a3) in enumerate(CLASSES):
-        here = (cls, pos[a2], pos[a1])
-        for d in (1, 3, 2):
-            dev = me + moved(a1, step_to(a1, d))
-            remote(tab, T.at[here], t1s.at[cls, d], t1r.at[cls, d], dev).start()
-            remote(cols(cls), G.at[here], g1s.at[cls, d], g1r.at[cls, d], dev).start()
-    for cls, (a1, a2, a3) in enumerate(CLASSES):
-        here = (cls, pos[a2], pos[a1])
-        spread(cls, 0, tab, cols(cls), pos[a1])
-        local(tab, T.at[here], t1r.at[cls, 0]).start()
-        local(cols(cls), G.at[here], g1r.at[cls, 0]).start()
+            remote(src, G.at[cls, g, pos[a2], to], g2s.at[cls, g, k, d], g2r.at[cls, g, k, d],
+                   me + moved(a2, step_to(a2, d))).start()
+
+    for g in range(2):
+        for cls, (a1, a2, a3) in enumerate(CLASSES):
+            for d in (1, 3, 2):
+                dev = me + moved(a1, step_to(a1, d))
+                if g == 0:
+                    remote(tab, T.at[cls, pos[a2], pos[a1]], t1s.at[cls, d], t1r.at[cls, d], dev).start()
+                remote(cols(cls, g), G.at[cls, g, pos[a2], pos[a1]], g1s.at[cls, g, d], g1r.at[cls, g, d], dev).start()
+        for cls, (a1, a2, a3) in enumerate(CLASSES):
+            spread(cls, g, 0, cols(cls, g), pos[a1])
+            local(cols(cls, g), G.at[cls, g, pos[a2], pos[a1]], g1r.at[cls, g, 0]).start()
+            if g == 0:
+                local(tab, T.at[cls, pos[a2], pos[a1]], t1r.at[cls, 0]).start()
 
     gate = jax.nn.sigmoid(dot_t(x_ref[...], wr_ref[...]))
     num_experts = wr_ref.shape[0]
@@ -123,13 +131,20 @@
     route = ROUTE_SCALE * picked / jnp.maximum(jnp.sum(picked, axis=1, keepdims=True), 1e-30)
     route_rank = jnp.concatenate(three_parts(route) + (rank.astype(BF16),), axis=1)
 
-    for d in (3, 1, 2):
-        for cls, (a1, a2, a3) in enumerate(CLASSES):
-            owner = (pos[a1] + RING - d) % RING
-            here = (cls, pos[a2], owner)
-            local(tab, T.at[here], t1r.at[cls, d]).wait()
-            local(cols(cls), G.at[here], g1r.at[cls, d]).wait()
-            spread(cls, d, T.at[here], G.at[here], owner)
+    for g in range(2):
+        for d in (3, 1, 2):
+            for cls, (a1, a2, a3) in enumerate(CLASSES):
+                owner = (pos[a1] + RING - d) % RING
+                src = G.at[cls, g, pos[a2], owner]
+                local(cols(cls, g), src, g1r.at[cls, g, d]).wait()
+                spread(cls, g, d, src, owner)
+        if g == 0:
+            for cls, (a1, a2, a3) in enumerate(CLASSES):
+                for d in range(RING):
+                    local(tab, T.at[cls, 0, 0], t1r.at[cls, d]).wait()
+                row = T.at[cls, pos[a2]]
+                for d in (1, 3, 2):
+                    remote(row, row, t2s.at[cls, d], t2r.at[cls, d], me + moved(a2, step_to(a2, d))).start()
 
     si, sj = iota((4 * slots, 128), 0), iota((4 * slots, 128), 1)
     for cls, (a1, a2, a3) in enumerate(CLASSES):
@@ -160,19 +175,28 @@
     src_base = ((iota((rows, 128), 0) % 8) * tokens).astype(F32)
     lane = iota((rows, 128), 1).astype(F32)
     tabs, lines = [], []
+
+    def gathered(g):
+        for cls in range(3):
+            for k in range(RING):
+                for d in (1, 3, 2):
+                    local(cols(cls, g), G.at[cls, g, 0, 0], g2r.at[cls, g, k, d]).wait()
+            local(cols(cls, g), G.at[cls, g, 0, 0], g1r.at[cls, g, 0]).wait()
+
+    gathered(0)
     for cls, (a1, a2, a3) in enumerate(CLASSES):
-        for k in range(RING):
-            here = (cls, pos[a2], pos[a1])
-            for d in (1, 3, 2):
-                local(tab, T.at[here], t2r.at[cls, k, d]).wait()
-                local(cols(cls), G.at[here], g2r.at[cls, k, d]).wait()
-        local(tab, T.at[here], t1r.at[cls, 0]).wait()
-        local(cols(cls), G.at[here], g1r.at[cls, 0]).wait()
+        for d in (1, 3, 2):
+            local(T.at[cls, 0], T.at[cls, 0], t2r.at[cls, d]).wait()
         tabs.append([dot(m, T[cls].reshape(256, slots)).astype(BF16) for m in by_rank])
         lines.append(me - core - pos[a3] * STRIDE[a3])
 
-    def select(i, _):
-        e, p = i // 2, i % 2
+    def select(n, _):
+        g, e, p = n // 2 % 2, n // 4, n % 2
+
+        @pl.when(n == 2)
+        def _():
+            gathered(1)
+
         for cls, (a1, a2, a3) in enumerate(CLASSES):
             picks = []
             for q in range(2):
@@ -187,28 +211,30 @@
                     for b in range(8 * tokens // 128):
                         Pm[cls, h, q * rows:(q + 1) * rows, b * 128:(b + 1) * 128] = (
                             jnp.where(code == lane + float(b * 128), 1.0, 0.0))
-                out = dot(Pm[cls, h].astype(BF16), G[cls, 2 * h:2 * h + 2].reshape(8 * tokens, third))
-                outs.append(out.reshape(2, CAP, 8, third))
+                out = dot(Pm[cls, h].astype(BF16), G[cls, g, 2 * h:2 * h + 2].reshape(8 * tokens, sixth))
+                outs.append(out.reshape(2, CAP, 8, sixth))
             both = jnp.concatenate(outs, axis=2).astype(BF16)
             for q in range(2):
                 d = 2 + q - p * (1 + 2 * q)
                 k = 2 * d + e
-                Sb[cls, k] = both[q]
+                Sb[cls, g, k] = both[q]
                 dev = me + moved(a3, step_to(a3, d)) + (core + e) % 2 - core
-                src, dst = Sb.at[cls, k], R.at[cls, pl.ds(core * CAP, CAP), pos[a3]]
+                src, dst = Sb.at[cls, g, k], R.at[cls, g, pl.ds(core * CAP, CAP), pos[a3]]
                 if q == 1:
-                    @pl.when(i == 1)
+                    mine = jnp.logical_and(n < 4, n % 2 == 1)
+
+                    @pl.when(mine)
                     def _():
-                        local(src, dst, d3r.at[cls, k]).start()
-
-                    @pl.when(i != 1)
+                        local(src, dst, d3r.at[cls, g, k]).start()
+
+                    @pl.when(jnp.logical_not(mine))
                     def _():
-                        remote(src, dst, d3s.at[cls, k], d3r.at[cls, k], dev).start()
+                        remote(src, dst, d3s.at[cls, g, k], d3r.at[cls, g, k], dev).start()
                 else:
-                    remote(src, dst, d3s.at[cls, k], d3r.at[cls, k], dev).start()
+                    remote(src, dst, d3s.at[cls, g, k], d3r.at[cls, g, k], dev).start()
         return 0
 
-    lax.fori_loop(0, RING, select, 0)
+    lax.fori_loop(0, 2 * RING, select, 0)
 
     for c in weight_copies[3:]:
         c.wait()
@@ -235,10 +261,11 @@
         half = (core + e) % 2
         for cls in range(3):
             for d in range(RING):
-                local(Sb.at[cls, 0], Sb.at[cls, 0], d3r.at[cls, 2 * d + e]).wait()
+                for g in range(2):
+                    local(Sb.at[cls, g, 0], Sb.at[cls, g, 0], d3r.at[cls, g, 2 * d + e]).wait()
         n = CAP * 64
-        xs = jnp.concatenate([permuted(to_first, cls, R[cls, pl.ds(half * CAP, CAP)].reshape(n, third))
-                              for cls in range(3)], axis=1)
+        xs = jnp.concatenate([permuted(to_first, cls, R[cls, g, pl.ds(half * CAP, CAP)].reshape(n, sixth))
+                              for cls in range(3) for g in range(2)], axis=1)
         mid = (jax.nn.silu(dot(xs, w1[...])) * dot(xs, w3[...])).astype(BF16)
         for cls, (a1, a2, a3) in enumerate(CLASSES):
             out = dot(mid, w2[:, cls * third:(cls + 1) * third]).astype(BF16)
@@ -261,6 +288,7 @@
         return 0
 
     lax.fori_loop(0, 2, expert, 0)
+    piece = Z.at[0, 0, :, 0]
 
     u2, v3 = pi // 16 % 4, pi // 4 % 4
     by_second = as_onehot(pj == pi // 64 * 64 + v3 * 16 + u2 * 4 + pi % 4)
@@ -269,13 +297,13 @@
         half = (core + e) % 2
         for cls, (a1, a2, a3) in enumerate(CLASSES):
             for d in range(RING):
-                local(Sb.at[cls, 0], Sb.at[cls, 0], d5r.at[cls, 2 * d + e]).wait()
+                local(piece, piece, d5r.at[cls, 2 * d + e]).wait()
             rows_in = Hb[cls, half].reshape(CAP * 64, third)
             Z[cls, half] = jnp.concatenate([dot(by_second, rows_in[i:i + blk]).astype(BF16) for i in
                                             range(0, CAP * 64, blk)], axis=0).reshape(CAP, RING, 16, third)
             for d in (2, 1, 3, 0):
                 v = step_to(a2, d)
-                src, dst = Z.at[cls, half, :, v], F.at[cls, :, pos[a2], half]
+                src, dst = Z.at[cls, half, :, v], F.at[cls, half, :, pos[a2]]
                 if d == 0:
                     local(src, dst, d6r.at[cls, e, d]).start()
                 else:
@@ -284,54 +312,74 @@
 
     lax.fori_loop(0, 2, regroup, 0)
 
-    all_tok = RING * tokens
-    ei, ej = iota((128, 128), 0), iota((128, 128), 1)
-    spreads = [as_onehot(ei == ej // 4 + 32 * part) for part in range(4)]
-    same = iota((all_tok, 128), 0) // tokens == iota((all_tok, 128), 1) % 4
-    for cls, (a1, a2, a3) in enumerate(CLASSES):
+    for cls in range(3):
         for d in range(RING):
             local(Cs.at[cls, 0], Cr.at[cls, 0], cr.at[cls, d]).wait()
-        c_all = Cr[cls].reshape(all_tok, 128)
-        w_exp = [dot(c_all, spreads[part]) for part in range(3)]
-        rank_exp = jnp.where(same, dot(c_all, spreads[3]), 99.0)
-        for e in range(2):
-            for d in range(RING):
-                local(Sb.at[cls, 0], Sb.at[cls, 0], d6r.at[cls, e, d]).wait()
-        acc = jnp.zeros((3 * all_tok, third), F32)
-        for r0 in range(0, CAP, 2):
-            ranks = range(r0, min(r0 + 2, CAP))
-            w = jnp.concatenate([jnp.concatenate([jnp.where(rank_exp == float(r), w_exp[part], 0.0) for r in ranks], axis=1)
-                                 for part in range(3)], axis=0).astype(BF16)
-            acc = acc + dot(w, F[cls, r0:r0 + len(ranks)].reshape(128 * len(ranks), third))
-        U[cls] = (acc[2 * all_tok:] + acc[all_tok:2 * all_tok] + acc[:all_tok]).reshape(RING, tokens, third)
-        for d in (2, 1, 3, 0):
-            v = step_to(a1, d)
-            if d == 0:
-                local(U.at[cls, v], A.at[cls, pos[a1]], d7r.at[cls, d]).start()
-            else:
-                remote(U.at[cls, v], A.at[cls, pos[a1]], d7s.at[cls, d], d7r.at[cls, d], me + moved(a1, v)).start()
+
+    def spreads(half):
+        ei, ej = iota((128, 256), 0), iota((128, 256), 1)
+        q = ej // 16 % 4 * 8 + half * 4 + ej // 4 % 4
+        return [as_onehot(ei == q + 32 * part) for part in range(4)]
+
+    def weigh(cls, half, spread_mats, targets):
+        m = tokens * len(targets)
+        lane_pos = iota((m, 256), 1)
+        c = jnp.concatenate([Cr[cls, v] for v in targets], axis=0)
+        w_exp = [dot(c, spread_mats[part]) for part in range(3)]
+        source = jnp.concatenate([jnp.full((tokens, 256), v, jnp.int32) for v in targets], axis=0)
+        rank_exp = jnp.where(lane_pos % 4 == source, dot(c, spread_mats[3]) - (lane_pos // 64).astype(F32), 99.0)
+        acc = jnp.zeros((3 * m, third), F32)
+        for r0 in range(0, CAP, 4):
+            k = 64 * min(4, CAP - r0)
+            hit = rank_exp == float(r0)
+            w = jnp.concatenate([jnp.where(hit, w_exp[part], 0.0) for part in range(3)], axis=0).astype(BF16)
+            acc = acc + dot(w[:, :k], F[cls, half, r0:r0 + k // 64].reshape(k, third))
+        return (acc[2 * m:] + acc[m:2 * m] + acc[:m]).reshape(len(targets), tokens, third)
+
+    def arrived(cls, e):
+        for d in range(RING):
+            local(piece, piece, d6r.at[cls, e, d]).wait()
+
+    mats = spreads(core)
     for cls in range(3):
-        for d in range(RING):
+        arrived(cls, 0)
+        U[cls] = weigh(cls, core, mats, list(range(RING)))
+    mats = spreads(1 - core)
+    for group in ((2,), (1, 3), (0,)):
+        for cls, (a1, a2, a3) in enumerate(CLASSES):
+            if group == (2,):
+                arrived(cls, 1)
+            targets = [step_to(a1, d) for d in group]
+            part = weigh(cls, 1 - core, mats, targets)
+            for i, (d, v) in enumerate(zip(group, targets)):
+                if d == 0:
+                    A[cls, pos[a1]] = U[cls, v] + part[i]
+                else:
+                    U[cls, v] = U[cls, v] + part[i]
+                    remote(U.at[cls, v], A.at[cls, pos[a1]], d7s.at[cls, d], d7r.at[cls, d], me + moved(a1, v)).start()
+    for cls in range(3):
+        for d in range(1, RING):
             local(U.at[cls, 0], A.at[cls, 0], d7r.at[cls, d]).wait()
         routed = (A[cls, 0] + A[cls, 1]) + (A[cls, 2] + A[cls, 3])
         y_ref[:, cls * third:(cls + 1) * third] = (zs[:, cls * third:(cls + 1) * third] + routed).astype(BF16)
 
-    for cls, (a1, a2, a3) in enumerate(CLASSES):
-        here = (cls, pos[a2], pos[a1])
+    for cls in range(3):
         for d in range(1, RING):
-            local(tab, T.at[here], t1s.at[cls, d]).wait()
-            local(cols(cls), G.at[here], g1s.at[cls, d]).wait()
+            local(tab, T.at[cls, 0, 0], t1s.at[cls, d]).wait()
+            local(T.at[cls, 0], T.at[cls, 0], t2s.at[cls, d]).wait()
             local(Cs.at[cls, 0], Cr.at[cls, 0], cs.at[cls, d]).wait()
-            for k in range(RING):
-                local(tab, T.at[here], t2s.at[cls, k, d]).wait()
-                local(cols(cls), G.at[here], g2s.at[cls, k, d]).wait()
+            for g in range(2):
+                local(cols(cls, g), G.at[cls, g, 0, 0], g1s.at[cls, g, d]).wait()
+                for k in range(RING):
+                    local(cols(cls, g), G.at[cls, g, 0, 0], g2s.at[cls, g, k, d]).wait()
         for k in range(1, 8):
-            local(Sb.at[cls, 0], Sb.at[cls, 0], d3s.at[cls, k]).wait()
-            local(Sb.at[cls, 0], Sb.at[cls, 0], d5s.at[cls, k]).wait()
+            for g in range(2):
+                local(Sb.at[cls, g, 0], Sb.at[cls, g, 0], d3s.at[cls, g, k]).wait()
+            local(piece, piece, d5s.at[cls, k]).wait()
         for d in range(1, RING):
             local(U.at[cls, 0], A.at[cls, 0], d7s.at[cls, d]).wait()
             for e in range(2):
-                local(Sb.at[cls, 0], Sb.at[cls, 0], d6s.at[cls, e, d]).wait()
+                local(piece, piece, d6s.at[cls, e, d]).wait()
 
 
 def solution(mesh):
@@ -346,29 +394,30 @@
         return pl.pallas_call(
             moe_kernel,
             out_shape=jax.ShapeDtypeStruct((tokens, dim), BF16),
-            in_specs=[vmem] * 4 + [hbm] * 6,
+            in_specs=[hbm] * 10,
             out_specs=vmem,
             scratch_shapes=[
-                V((3, RING, RING, tokens, third), BF16),
+                V((tokens, dim), BF16), V(assign.T.shape, jnp.int32), V((1, slots), jnp.int32), V(w_router.T.shape, BF16),
+                V((3, 2, RING, RING, tokens, third // 2), BF16),
                 V((3, RING, RING, 16, slots), BF16),
                 V((16, slots), BF16),
                 V((3, 2, 2 * CAP * 8, 8 * tokens), F32),
-                V((3, 8, CAP, 16, third), BF16),
-                V((3, 2 * CAP, RING, 16, third), BF16),
+                V((3, 2, 8, CAP, 16, third // 2), BF16),
+                V((3, 2, 2 * CAP, RING, 16, third // 2), BF16),
                 V((3, 2 * CAP, RING, 16, third), BF16),
                 V((3, 2, CAP, RING, 16, third), BF16),
                 V((3, 2, CAP, RING, 16, third), BF16),
-                V((3, CAP, RING, 2, 16, third), BF16),
+                V((3, 2, CAP, RING, 16, third), BF16),
                 V((3, RING, tokens, 128), BF16), V((3, RING, tokens, 128), BF16),
                 V((3, RING, tokens, third), F32), V((3, RING, tokens, third), F32),
                 V((tokens, dim), F32),
                 V(w1_slots.shape[1:], BF16), V(w3_slots.shape[1:], BF16), V(w2_slots.shape[1:], BF16),
                 V(w1_shared.shape, BF16), V(w3_shared.shape, BF16), V(w2_shared.shape, BF16),
-                dma((6,)),
-                dma((3, 4)), dma((3, 4)), dma((3, 4, 4)), dma((3, 4, 4)),
-                dma((3, 4)), dma((3, 4)), dma((3, 4, 4)), dma((3, 4, 4)),
+                dma((6,)), dma((4,)),
+                dma((3, 2, 4)), dma((3, 2, 4)), dma((3, 2, 4, 4)), dma((3, 2, 4, 4)),
+                dma((3, 4)), dma((3, 4)), dma((3, 4)), dma((3, 4)),
                 dma((3, 4)), dma((3, 4)),
-                dma((3, 8)), dma((3, 8)), dma((3, 8)), dma((3, 8)),
+                dma((3, 2, 8)), dma((3, 2, 8)), dma((3, 8)), dma((3, 8)),
                 dma((3, 2, 4)), dma((3, 2, 4)), dma((3, 4)), dma((3, 4)),
             ],
             compiler_params=pltpu.CompilerParams(collective_id=0, has_side_effects=True,

time: 88.7 us -> 84.1 us (0.948)
  Pallas kernels: 86.9 us -> 82.3 us
    pallas_call x1, Pallas kernels: 86.9 us -> 82.3 us  [device_step(): pl.pallas_call(moe_kernel, out_shape=jax.ShapeDtypeStruct((tokens, dim),...]
where the time goes in v3:
time: 84.1 us; the launch traced here: 84 us
  Pallas kernels  82.3 us (98%)
  local copies, waits for them, and re-layouts  1.62 us (2%)
    pallas_call x1, Pallas kernels, device_step(): pl.pallas_call(moe_kernel, out_shape=jax.ShapeDtypeStruct((tokens, dim),...  82.3 us

profile of v3, /device:TPU:1, one launch (start us, length us, event | category | flops | bytes accessed | tf_op | source)
XLA Modules:
  0.0 84.0 jit_solution(18165904525782353010)
XLA Ops:
  0.0 82.3 %shard_map.100 = bf16[64,1536]{1,0:T(8,128)(2,1)} custom-call(bf16[64,1536]{1,0:T(8,128)(2,1)} %x_hbm.1, s32[6,64]{1,0:T(8,128)} %bitcast.4, s32[1,128]{1,0:T(1,128)} %bitcast.5, bf16[64,1536]{1,0:T(8,128)(2,1)} %bitcast.3, bf16[1,1536,512]{2,1,0:T(8,128)(2,1)} %w1_hbm.1, bf16[1,1536,512]{2,1,0:T(8,128)(2,1)} %w3_hbm.1, bf16[1,512,1536]{2,1,0:T(8,128)(2,1)} %w2_hbm.1, ...), custom_call_target="tpu_custom_call" | custom-call | tf_op jit(solution)/shard_map/pallas_call | solution.py:394
  82.3 1.6 %copy.12 = bf16[64,1536]{1,0:T(8,128)(2,1)} copy(bf16[64,1536]{1,0:T(8,128)(2,1)} %shard_map.100) | data formatting | bytes 393216

commit v4 on v3

--- a/solution.py
+++ b/solution.py
@@ -41,7 +41,8 @@
 def moe_kernel(x_hbm, assign_hbm, slot_expert_hbm, wr_hbm, w1_hbm, w3_hbm, w2_hbm, s1_hbm, s3_hbm, s2_hbm, y_ref,
                x_ref, assign_ref, slot_expert_ref, wr_ref,
                G, T, tab, Pm, Sb, R, Ob, Hb, Z, F, Cs, Cr, U, A, zs, w1, w3, w2, s1, s3, s2,
-               wsem, isem, g1s, g1r, g2s, g2r, t1s, t1r, t2s, t2r, cs, cr, d3s, d3r, d5s, d5r, d6s, d6r, d7s, d7r):
+               wsem, isem, sent, t1r, t2r, g0r, g1r, g2r, cr, d3r, d5r, d6r, d7r):
+    t1s, t2s, g1s, g2s, cs, d3s, d5s, d6s, d7s = (sent.at[i] for i in range(9))
     me = lax.axis_index('ep')
     core = me % 2
     pos = {'x': (me // 2) % RING, 'y': (me // 8) % RING, 'z': me // 32}
@@ -60,6 +61,9 @@
 
     def local(src, dst, sem):
         return pltpu.make_async_copy(src, dst, sem)
+
+    def wait_bytes(ref, sem):
+        pltpu.make_async_copy(ref, ref, sem).wait()
 
     barrier = pltpu.get_barrier_semaphore()
 
@@ -107,7 +111,7 @@
     def spread(cls, g, k, src, to):
         a2 = CLASSES[cls][1]
         for d in (1, 3, 2):
-            remote(src, G.at[cls, g, pos[a2], to], g2s.at[cls, g, k, d], g2r.at[cls, g, k, d],
+            remote(src, G.at[cls, g, pos[a2], to], g2s, g2r.at[g],
                    me + moved(a2, step_to(a2, d))).start()
 
     for g in range(2):
@@ -115,13 +119,13 @@
             for d in (1, 3, 2):
                 dev = me + moved(a1, step_to(a1, d))
                 if g == 0:
-                    remote(tab, T.at[cls, pos[a2], pos[a1]], t1s.at[cls, d], t1r.at[cls, d], dev).start()
-                remote(cols(cls, g), G.at[cls, g, pos[a2], pos[a1]], g1s.at[cls, g, d], g1r.at[cls, g, d], dev).start()
+                    remote(tab, T.at[cls, pos[a2], pos[a1]], t1s, t1r.at[0], dev).start()
+                remote(cols(cls, g), G.at[cls, g, pos[a2], pos[a1]], g1s, g1r.at[g, d - 1], dev).start()
         for cls, (a1, a2, a3) in enumerate(CLASSES):
             spread(cls, g, 0, cols(cls, g), pos[a1])
-            local(cols(cls, g), G.at[cls, g, pos[a2], pos[a1]], g1r.at[cls, g, 0]).start()
+            local(cols(cls, g), G.at[cls, g, pos[a2], pos[a1]], g0r.at[0]).start()
             if g == 0:
-                local(tab, T.at[cls, pos[a2], pos[a1]], t1r.at[cls, 0]).start()
+                T[cls, pos[a2], pos[a1]] = tab[...]
 
     gate = jax.nn.sigmoid(dot_t(x_ref[...], wr_ref[...]))
     num_experts = wr_ref.shape[0]
@@ -133,18 +137,16 @@
 
     for g in range(2):
         for d in (3, 1, 2):
+            wait_bytes(G.at[:, g, 0, 0], g1r.at[g, d - 1])
             for cls, (a1, a2, a3) in enumerate(CLASSES):
                 owner = (pos[a1] + RING - d) % RING
-                src = G.at[cls, g, pos[a2], owner]
-                local(cols(cls, g), src, g1r.at[cls, g, d]).wait()
-                spread(cls, g, d, src, owner)
+                spread(cls, g, d, G.at[cls, g, pos[a2], owner], owner)
         if g == 0:
+            wait_bytes(T.at[:, 0, 0:3], t1r.at[0])
             for cls, (a1, a2, a3) in enumerate(CLASSES):
-                for d in range(RING):
-                    local(tab, T.at[cls, 0, 0], t1r.at[cls, d]).wait()
                 row = T.at[cls, pos[a2]]
                 for d in (1, 3, 2):
-                    remote(row, row, t2s.at[cls, d], t2r.at[cls, d], me + moved(a2, step_to(a2, d))).start()
+                    remote(row, row, t2s, t2r.at[0], me + moved(a2, step_to(a2, d))).start()
 
     si, sj = iota((4 * slots, 128), 0), iota((4 * slots, 128), 1)
     for cls, (a1, a2, a3) in enumerate(CLASSES):
@@ -154,9 +156,9 @@
         for d in (1, 3, 2, 0):
             v = step_to(a1, d)
             if d == 0:
-                local(Cs.at[cls, v], Cr.at[cls, pos[a1]], cr.at[cls, d]).start()
+                Cr[cls, pos[a1]] = Cs[cls, v]
             else:
-                remote(Cs.at[cls, v], Cr.at[cls, pos[a1]], cs.at[cls, d], cr.at[cls, d], me + moved(a1, v)).start()
+                remote(Cs.at[cls, v], Cr.at[cls, pos[a1]], cs, cr.at[0], me + moved(a1, v)).start()
 
     for c in weight_copies[:3]:
         c.wait()
@@ -176,17 +178,10 @@
     lane = iota((rows, 128), 1).astype(F32)
     tabs, lines = [], []
 
-    def gathered(g):
-        for cls in range(3):
-            for k in range(RING):
-                for d in (1, 3, 2):
-                    local(cols(cls, g), G.at[cls, g, 0, 0], g2r.at[cls, g, k, d]).wait()
-            local(cols(cls, g), G.at[cls, g, 0, 0], g1r.at[cls, g, 0]).wait()
-
-    gathered(0)
+    wait_bytes(G.at[:, :, 0, 0], g0r.at[0])
+    wait_bytes(G.at[:, 0, 0:3], g2r.at[0])
+    wait_bytes(T.at[:, 0:3], t2r.at[0])
     for cls, (a1, a2, a3) in enumerate(CLASSES):
-        for d in (1, 3, 2):
-            local(T.at[cls, 0], T.at[cls, 0], t2r.at[cls, d]).wait()
         tabs.append([dot(m, T[cls].reshape(256, slots)).astype(BF16) for m in by_rank])
         lines.append(me - core - pos[a3] * STRIDE[a3])
 
@@ -195,7 +190,7 @@
 
         @pl.when(n == 2)
         def _():
-            gathered(1)
+            wait_bytes(G.at[:, 1, 0:3], g2r.at[1])
 
         for cls, (a1, a2, a3) in enumerate(CLASSES):
             picks = []
@@ -225,13 +220,13 @@
 
                     @pl.when(mine)
                     def _():
-                        local(src, dst, d3r.at[cls, g, k]).start()
+                        local(src, dst, d3r.at[e]).start()
 
                     @pl.when(jnp.logical_not(mine))
                     def _():
-                        remote(src, dst, d3s.at[cls, g, k], d3r.at[cls, g, k], dev).start()
+                        remote(src, dst, d3s, d3r.at[e], dev).start()
                 else:
-                    remote(src, dst, d3s.at[cls, g, k], d3r.at[cls, g, k], dev).start()
+                    remote(src, dst, d3s, d3r.at[e], dev).start()
         return 0
 
     lax.fori_loop(0, 2 * RING, select, 0)
@@ -259,10 +254,7 @@
 
     def expert(e, _):
         half = (core + e) % 2
-        for cls in range(3):
-            for d in range(RING):
-                for g in range(2):
-                    local(Sb.at[cls, g, 0], Sb.at[cls, g, 0], d3r.at[cls, g, 2 * d + e]).wait()
+        wait_bytes(R.at[:, :, 0:CAP], d3r.at[e])
         n = CAP * 64
         xs = jnp.concatenate([permuted(to_first, cls, R[cls, g, pl.ds(half * CAP, CAP)].reshape(n, sixth))
                               for cls in range(3) for g in range(2)], axis=1)
@@ -272,23 +264,21 @@
             Ob[cls, pl.ds(half * CAP, CAP)] = permuted(from_first, cls, out).reshape(CAP, RING, 16, third)
             for d in (2, 1, 3, 0):
                 v = step_to(a3, d)
-                k = 2 * d + e
                 dev = me + moved(a3, v) + half - core
                 src, dst = Ob.at[cls, pl.ds(half * CAP, CAP), v], Hb.at[cls, core, :, pos[a3]]
                 if d == 0:
                     @pl.when(e == 0)
                     def _():
-                        local(src, dst, d5r.at[cls, k]).start()
+                        local(src, dst, d5r.at[e, cls]).start()
 
                     @pl.when(e != 0)
                     def _():
-                        remote(src, dst, d5s.at[cls, k], d5r.at[cls, k], dev).start()
+                        remote(src, dst, d5s, d5r.at[e, cls], dev).start()
                 else:
-                    remote(src, dst, d5s.at[cls, k], d5r.at[cls, k], dev).start()
+                    remote(src, dst, d5s, d5r.at[e, cls], dev).start()
         return 0
 
     lax.fori_loop(0, 2, expert, 0)
-    piece = Z.at[0, 0, :, 0]
 
     u2, v3 = pi // 16 % 4, pi // 4 % 4
     by_second = as_onehot(pj == pi // 64 * 64 + v3 * 16 + u2 * 4 + pi % 4)
@@ -296,8 +286,7 @@
     def regroup(e, _):
         half = (core + e) % 2
         for cls, (a1, a2, a3) in enumerate(CLASSES):
-            for d in range(RING):
-                local(piece, piece, d5r.at[cls, 2 * d + e]).wait()
+            wait_bytes(Hb.at[cls, half], d5r.at[e, cls])
             rows_in = Hb[cls, half].reshape(CAP * 64, third)
             Z[cls, half] = jnp.concatenate([dot(by_second, rows_in[i:i + blk]).astype(BF16) for i in
                                             range(0, CAP * 64, blk)], axis=0).reshape(CAP, RING, 16, third)
@@ -305,16 +294,14 @@
                 v = step_to(a2, d)
                 src, dst = Z.at[cls, half, :, v], F.at[cls, half, :, pos[a2]]
                 if d == 0:
-                    local(src, dst, d6r.at[cls, e, d]).start()
+                    local(src, dst, d6r.at[e, cls]).start()
                 else:
-                    remote(src, dst, d6s.at[cls, e, d], d6r.at[cls, e, d], me + moved(a2, v)).start()
+                    remote(src, dst, d6s, d6r.at[e, cls], me + moved(a2, v)).start()
         return 0
 
     lax.fori_loop(0, 2, regroup, 0)
 
-    for cls in range(3):
-        for d in range(RING):
-            local(Cs.at[cls, 0], Cr.at[cls, 0], cr.at[cls, d]).wait()
+    wait_bytes(Cr.at[:, 0:3], cr.at[0])
 
     def spreads(half):
         ei, ej = iota((128, 256), 0), iota((128, 256), 1)
@@ -336,19 +323,15 @@
             acc = acc + dot(w[:, :k], F[cls, half, r0:r0 + k // 64].reshape(k, third))
         return (acc[2 * m:] + acc[m:2 * m] + acc[:m]).reshape(len(targets), tokens, third)
 
-    def arrived(cls, e):
-        for d in range(RING):
-            local(piece, piece, d6r.at[cls, e, d]).wait()
-
     mats = spreads(core)
     for cls in range(3):
-        arrived(cls, 0)
+        wait_bytes(F.at[cls, core], d6r.at[0, cls])
         U[cls] = weigh(cls, core, mats, list(range(RING)))
     mats = spreads(1 - core)
     for group in ((2,), (1, 3), (0,)):
         for cls, (a1, a2, a3) in enumerate(CLASSES):
             if group == (2,):
-                arrived(cls, 1)
+                wait_bytes(F.at[cls, 1 - core], d6r.at[1, cls])
             targets = [step_to(a1, d) for d in group]
             part = weigh(cls, 1 - core, mats, targets)
             for i, (d, v) in enumerate(zip(group, targets)):
@@ -356,30 +339,16 @@
                     A[cls, pos[a1]] = U[cls, v] + part[i]
                 else:
                     U[cls, v] = U[cls, v] + part[i]
-                    remote(U.at[cls, v], A.at[cls, pos[a1]], d7s.at[cls, d], d7r.at[cls, d], me + moved(a1, v)).start()
+                    remote(U.at[cls, v], A.at[cls, pos[a1]], d7s, d7r.at[cls], me + moved(a1, v)).start()
     for cls in range(3):
-        for d in range(1, RING):
-            local(U.at[cls, 0], A.at[cls, 0], d7r.at[cls, d]).wait()
+        wait_bytes(A.at[cls, 0:3], d7r.at[cls])
         routed = (A[cls, 0] + A[cls, 1]) + (A[cls, 2] + A[cls, 3])
         y_ref[:, cls * third:(cls + 1) * third] = (zs[:, cls * third:(cls + 1) * third] + routed).astype(BF16)
 
-    for cls in range(3):
-        for d in range(1, RING):
-            local(tab, T.at[cls, 0, 0], t1s.at[cls, d]).wait()
-            local(T.at[cls, 0], T.at[cls, 0], t2s.at[cls, d]).wait()
-            local(Cs.at[cls, 0], Cr.at[cls, 0], cs.at[cls, d]).wait()
-            for g in range(2):
-                local(cols(cls, g), G.at[cls, g, 0, 0], g1s.at[cls, g, d]).wait()
-                for k in range(RING):
-                    local(cols(cls, g), G.at[cls, g, 0, 0], g2s.at[cls, g, k, d]).wait()
-        for k in range(1, 8):
-            for g in range(2):
-                local(Sb.at[cls, g, 0], Sb.at[cls, g, 0], d3s.at[cls, g, k]).wait()
-            local(piece, piece, d5s.at[cls, k]).wait()
-        for d in range(1, RING):
-            local(U.at[cls, 0], A.at[cls, 0], d7s.at[cls, d]).wait()
-            for e in range(2):
-                local(piece, piece, d6s.at[cls, e, d]).wait()
+    for ref, sem in ((T.at[:, 0, 0:3], t1s), (T.at[:, 0:3], t2s), (G.at[:, :, 0, 0:3], g1s), (G.at[:, :, 0:3], g2s),
+                     (Cs.at[:, 0:3], cs), (Sb.at[:, :, 0:7], d3s), (Sb.at[:, :, 0:7], d5s), (Z.at[:, :, :, 0:3], d6s),
+                     (U.at[:, 0:3], d7s)):
+        wait_bytes(ref, sem)
 
 
 def solution(mesh):
@@ -413,12 +382,8 @@
                 V((tokens, dim), F32),
                 V(w1_slots.shape[1:], BF16), V(w3_slots.shape[1:], BF16), V(w2_slots.shape[1:], BF16),
                 V(w1_shared.shape, BF16), V(w3_shared.shape, BF16), V(w2_shared.shape, BF16),
-                dma((6,)), dma((4,)),
-                dma((3, 2, 4)), dma((3, 2, 4)), dma((3, 2, 4, 4)), dma((3, 2, 4, 4)),
-                dma((3, 4)), dma((3, 4)), dma((3, 4)), dma((3, 4)),
-                dma((3, 4)), dma((3, 4)),
-                dma((3, 2, 8)), dma((3, 2, 8)), dma((3, 8)), dma((3, 8)),
-                dma((3, 2, 4)), dma((3, 2, 4)), dma((3, 4)), dma((3, 4)),
+                dma((6,)), dma((4,)), dma((9,)), dma((1,)), dma((1,)), dma((1,)), dma((2, 3)), dma((2,)), dma((1,)),
+                dma((2,)), dma((2, 3)), dma((2, 3)), dma((3,)),
             ],
             compiler_params=pltpu.CompilerParams(collective_id=0, has_side_effects=True,
                                                  vmem_limit_bytes=60 * 2 ** 20),

time: 84.1 us -> 79.4 us (0.944)
  Pallas kernels: 82.3 us -> 77.6 us
    pallas_call x1, Pallas kernels: 82.3 us -> 77.6 us  [device_step(): pl.pallas_call(moe_kernel, out_shape=jax.ShapeDtypeStruct((tokens, dim),...]
where the time goes in v4:
time: 79.4 us; the launch traced here: 79.2 us
  Pallas kernels  77.6 us (98%)
  local copies, waits for them, and re-layouts  1.62 us (2%)
    pallas_call x1, Pallas kernels, device_step(): pl.pallas_call(moe_kernel, out_shape=jax.ShapeDtypeStruct((tokens, dim),...  77.6 us
    unnamed x1, local copies, waits for them, and re-layouts  1.62 us

profile of v4, /device:TPU:1, one launch (start us, length us, event | category | flops | bytes accessed | tf_op | source)
XLA Modules:
  0.0 79.2 jit_solution(14944294307566559420)
XLA Ops:
  0.0 77.6 %shard_map.100 = bf16[64,1536]{1,0:T(8,128)(2,1)} custom-call(bf16[64,1536]{1,0:T(8,128)(2,1)} %x_hbm.1, s32[6,64]{1,0:T(8,128)} %bitcast.4, s32[1,128]{1,0:T(1,128)} %bitcast.5, bf16[64,1536]{1,0:T(8,128)(2,1)} %bitcast.3, bf16[1,1536,512]{2,1,0:T(8,128)(2,1)} %w1_hbm.1, bf16[1,1536,512]{2,1,0:T(8,128)(2,1)} %w3_hbm.1, bf16[1,512,1536]{2,1,0:T(8,128)(2,1)} %w2_hbm.1, ...), custom_call_target="tpu_custom_call" | custom-call | tf_op jit(solution)/shard_map/pallas_call | solution.py:363
  77.6 1.6 %copy.12 = bf16[64,1536]{1,0:T(8,128)(2,1)} copy(bf16[64,1536]{1,0:T(8,128)(2,1)} %shard_map.100) | data formatting | bytes 393216

commit v5 on v4

--- a/solution.py
+++ b/solution.py
@@ -41,7 +41,7 @@
 def moe_kernel(x_hbm, assign_hbm, slot_expert_hbm, wr_hbm, w1_hbm, w3_hbm, w2_hbm, s1_hbm, s3_hbm, s2_hbm, y_ref,
                x_ref, assign_ref, slot_expert_ref, wr_ref,
                G, T, tab, Pm, Sb, R, Ob, Hb, Z, F, Cs, Cr, U, A, zs, w1, w3, w2, s1, s3, s2,
-               wsem, isem, sent, t1r, t2r, g0r, g1r, g2r, cr, d3r, d5r, d6r, d7r):
+               wsem, isem, sent, t1r, t2r, g0r, g1r, g2r, gfr, cr, d3r, d5r, d6r, d7r):
     t1s, t2s, g1s, g2s, cs, d3s, d5s, d6s, d7s = (sent.at[i] for i in range(9))
     me = lax.axis_index('ep')
     core = me % 2
@@ -110,9 +110,17 @@
 
     def spread(cls, g, k, src, to):
         a2 = CLASSES[cls][1]
-        for d in (1, 3, 2):
-            remote(src, G.at[cls, g, pos[a2], to], g2s, g2r.at[g],
+        for d in (1, 3):
+            passed_on = (k % 2 == 0) == (d == 1)
+            remote(src, G.at[cls, g, pos[a2], to], g2s, gfr.at[g, k] if passed_on else g2r.at[g],
                    me + moved(a2, step_to(a2, d))).start()
+
+    def pass_on(g, k):
+        wait_bytes(G.at[:, g, 0, 0], gfr.at[g, k])
+        d = 1 if k % 2 == 0 else 3
+        for cls, (a1, a2, a3) in enumerate(CLASSES):
+            block = G.at[cls, g, step_to(a2, RING - d), step_to(a1, RING - k)]
+            remote(block, block, g2s, g2r.at[g], me + moved(a2, step_to(a2, d))).start()
 
     for g in range(2):
         for cls, (a1, a2, a3) in enumerate(CLASSES):
@@ -139,8 +147,12 @@
         for d in (3, 1, 2):
             wait_bytes(G.at[:, g, 0, 0], g1r.at[g, d - 1])
             for cls, (a1, a2, a3) in enumerate(CLASSES):
-                owner = (pos[a1] + RING - d) % RING
+                owner = step_to(a1, RING - d)
                 spread(cls, g, d, G.at[cls, g, pos[a2], owner], owner)
+            if d == 1:
+                pass_on(g, 0)
+        for k in (3, 1, 2):
+            pass_on(g, k)
         if g == 0:
             wait_bytes(T.at[:, 0, 0:3], t1r.at[0])
             for cls, (a1, a2, a3) in enumerate(CLASSES):
@@ -179,7 +191,7 @@
     tabs, lines = [], []
 
     wait_bytes(G.at[:, :, 0, 0], g0r.at[0])
-    wait_bytes(G.at[:, 0, 0:3], g2r.at[0])
+    wait_bytes(G.at[:, 0, 0:2], g2r.at[0])
     wait_bytes(T.at[:, 0:3], t2r.at[0])
     for cls, (a1, a2, a3) in enumerate(CLASSES):
         tabs.append([dot(m, T[cls].reshape(256, slots)).astype(BF16) for m in by_rank])
@@ -190,7 +202,7 @@
 
         @pl.when(n == 2)
         def _():
-            wait_bytes(G.at[:, 1, 0:3], g2r.at[1])
+            wait_bytes(G.at[:, 1, 0:2], g2r.at[1])
 
         for cls, (a1, a2, a3) in enumerate(CLASSES):
             picks = []
@@ -290,13 +302,14 @@
             rows_in = Hb[cls, half].reshape(CAP * 64, third)
             Z[cls, half] = jnp.concatenate([dot(by_second, rows_in[i:i + blk]).astype(BF16) for i in
                                             range(0, CAP * 64, blk)], axis=0).reshape(CAP, RING, 16, third)
-            for d in (2, 1, 3, 0):
+            for g, d in [(g, d) for g in range(2) for d in (2, 1, 3, 0)]:
                 v = step_to(a2, d)
-                src, dst = Z.at[cls, half, :, v], F.at[cls, half, :, pos[a2]]
+                part = pl.ds(g * sixth, sixth)
+                src, dst = Z.at[cls, half, :, v, :, part], F.at[cls, half, :, pos[a2], :, part]
                 if d == 0:
-                    local(src, dst, d6r.at[e, cls]).start()
+                    local(src, dst, d6r.at[e, g, cls]).start()
                 else:
-                    remote(src, dst, d6s, d6r.at[e, cls], me + moved(a2, v)).start()
+                    remote(src, dst, d6s, d6r.at[e, g, cls], me + moved(a2, v)).start()
         return 0
 
     lax.fori_loop(0, 2, regroup, 0)
@@ -308,42 +321,50 @@
         q = ej // 16 % 4 * 8 + half * 4 + ej // 4 % 4
         return [as_onehot(ei == q + 32 * part) for part in range(4)]
 
-    def weigh(cls, half, spread_mats, targets):
+    def weigh(cls, half, spread_mats, targets, first, width):
         m = tokens * len(targets)
         lane_pos = iota((m, 256), 1)
         c = jnp.concatenate([Cr[cls, v] for v in targets], axis=0)
         w_exp = [dot(c, spread_mats[part]) for part in range(3)]
         source = jnp.concatenate([jnp.full((tokens, 256), v, jnp.int32) for v in targets], axis=0)
         rank_exp = jnp.where(lane_pos % 4 == source, dot(c, spread_mats[3]) - (lane_pos // 64).astype(F32), 99.0)
-        acc = jnp.zeros((3 * m, third), F32)
+        acc = jnp.zeros((3 * m, width), F32)
         for r0 in range(0, CAP, 4):
             k = 64 * min(4, CAP - r0)
             hit = rank_exp == float(r0)
             w = jnp.concatenate([jnp.where(hit, w_exp[part], 0.0) for part in range(3)], axis=0).astype(BF16)
-            acc = acc + dot(w[:, :k], F[cls, half, r0:r0 + k // 64].reshape(k, third))
-        return (acc[2 * m:] + acc[m:2 * m] + acc[:m]).reshape(len(targets), tokens, third)
+            acc = acc + dot(w[:, :k], F[cls, half, r0:r0 + k // 64, :, :, first:first + width].reshape(k, width))
+        return (acc[2 * m:] + acc[m:2 * m] + acc[:m]).reshape(len(targets), tokens, width)
 
     mats = spreads(core)
     for cls in range(3):
-        wait_bytes(F.at[cls, core], d6r.at[0, cls])
-        U[cls] = weigh(cls, core, mats, list(range(RING)))
+        for g in range(2):
+            wait_bytes(F.at[cls, core, :, :, :, 0:sixth], d6r.at[0, g, cls])
+        U[cls] = weigh(cls, core, mats, list(range(RING)), 0, third)
     mats = spreads(1 - core)
-    for group in ((2,), (1, 3), (0,)):
-        for cls, (a1, a2, a3) in enumerate(CLASSES):
-            if group == (2,):
-                wait_bytes(F.at[cls, 1 - core], d6r.at[1, cls])
-            targets = [step_to(a1, d) for d in group]
-            part = weigh(cls, 1 - core, mats, targets)
-            for i, (d, v) in enumerate(zip(group, targets)):
-                if d == 0:
-                    A[cls, pos[a1]] = U[cls, v] + part[i]
-                else:
-                    U[cls, v] = U[cls, v] + part[i]
-                    remote(U.at[cls, v], A.at[cls, pos[a1]], d7s, d7r.at[cls], me + moved(a1, v)).start()
-    for cls in range(3):
-        wait_bytes(A.at[cls, 0:3], d7r.at[cls])
-        routed = (A[cls, 0] + A[cls, 1]) + (A[cls, 2] + A[cls, 3])
-        y_ref[:, cls * third:(cls + 1) * third] = (zs[:, cls * third:(cls + 1) * third] + routed).astype(BF16)
+    for g in range(2):
+        here = slice(g * sixth, (g + 1) * sixth)
+        part = pl.ds(g * sixth, sixth)
+        for group in ((2,), (1, 3), (0,)):
+            for cls, (a1, a2, a3) in enumerate(CLASSES):
+                if group == (2,):
+                    wait_bytes(F.at[cls, 1 - core, :, :, :, 0:sixth], d6r.at[1, g, cls])
+                targets = [step_to(a1, d) for d in group]
+                added = weigh(cls, 1 - core, mats, targets, g * sixth, sixth)
+                for i, (d, v) in enumerate(zip(group, targets)):
+                    if d == 0:
+                        A[cls, pos[a1], :, here] = U[cls, v, :, here] + added[i]
+                    else:
+                        U[cls, v, :, here] = U[cls, v, :, here] + added[i]
+                        remote(U.at[cls, v, :, part], A.at[cls, pos[a1], :, part], d7s, d7r.at[g, cls],
+                               me + moved(a1, v)).start()
+    for g in range(2):
+        for cls in range(3):
+            wait_bytes(A.at[cls, 0:3, :, 0:sixth], d7r.at[g, cls])
+            here = slice(g * sixth, (g + 1) * sixth)
+            there = slice((2 * cls + g) * sixth, (2 * cls + g + 1) * sixth)
+            routed = (A[cls, 0, :, here] + A[cls, 1, :, here]) + (A[cls, 2, :, here] + A[cls, 3, :, here])
+            y_ref[:, there] = (zs[:, there] + routed).astype(BF16)
 
     for ref, sem in ((T.at[:, 0, 0:3], t1s), (T.at[:, 0:3], t2s), (G.at[:, :, 0, 0:3], g1s), (G.at[:, :, 0:3], g2s),
                      (Cs.at[:, 0:3], cs), (Sb.at[:, :, 0:7], d3s), (Sb.at[:, :, 0:7], d5s), (Z.at[:, :, :, 0:3], d6s),
@@ -382,8 +403,8 @@
                 V((tokens, dim), F32),
                 V(w1_slots.shape[1:], BF16), V(w3_slots.shape[1:], BF16), V(w2_slots.shape[1:], BF16),
                 V(w1_shared.shape, BF16), V(w3_shared.shape, BF16), V(w2_shared.shape, BF16),
-                dma((6,)), dma((4,)), dma((9,)), dma((1,)), dma((1,)), dma((1,)), dma((2, 3)), dma((2,)), dma((1,)),
-                dma((2,)), dma((2, 3)), dma((2, 3)), dma((3,)),
+                dma((6,)), dma((4,)), dma((9,)), dma((1,)), dma((1,)), dma((1,)), dma((2, 3)), dma((2,)), dma((2, 4)), dma((1,)),
+                dma((2,)), dma((2, 3)), dma((2, 2, 3)), dma((2, 3)),
             ],
             compiler_params=pltpu.CompilerParams(collective_id=0, has_side_effects=True,
                                                  vmem_limit_bytes=60 * 2 ** 20),

time: 79.4 us -> 82.2 us (1.035)
  Pallas kernels: 77.6 us -> 80.4 us
    pallas_call x1, Pallas kernels: 77.6 us -> 80.4 us  [device_step(): pl.pallas_call(moe_kernel, out_shape=jax.ShapeDtypeStruct((tokens, dim),...]
where the time goes in v5:
time: 82.2 us; the launch traced here: 82 us
  Pallas kernels  80.4 us (98%)
  local copies, waits for them, and re-layouts  1.62 us (2%)
    pallas_call x1, Pallas kernels, device_step(): pl.pallas_call(moe_kernel, out_shape=jax.ShapeDtypeStruct((tokens, dim),...  80.4 us

profile of v5, /device:TPU:1, one launch (start us, length us, event | category | flops | bytes accessed | tf_op | source)
XLA Modules:
  0.0 82.0 jit_solution(4977546285365756606)
XLA Ops:
  0.0 80.4 %shard_map.100 = bf16[64,1536]{1,0:T(8,128)(2,1)} custom-call(bf16[64,1536]{1,0:T(8,128)(2,1)} %x_hbm.1, s32[6,64]{1,0:T(8,128)} %bitcast.4, s32[1,128]{1,0:T(1,128)} %bitcast.5, bf16[64,1536]{1,0:T(8,128)(2,1)} %bitcast.3, bf16[1,1536,512]{2,1,0:T(8,128)(2,1)} %w1_hbm.1, bf16[1,1536,512]{2,1,0:T(8,128)(2,1)} %w3_hbm.1, bf16[1,512,1536]{2,1,0:T(8,128)(2,1)} %w2_hbm.1, ...), custom_call_target="tpu_custom_call" | custom-call | tf_op jit(solution)/shard_map/pallas_call | solution.py:384
  80.4 1.6 %copy.12 = bf16[64,1536]{1,0:T(8,128)(2,1)} copy(bf16[64,1536]{1,0:T(8,128)(2,1)} %shard_map.100) | data formatting | bytes 393216

commit v6 on v4

--- a/solution.py
+++ b/solution.py
@@ -82,8 +82,13 @@
         ((assign_hbm, assign_ref), (x_hbm, x_ref), (slot_expert_hbm, slot_expert_ref), (wr_hbm, wr_ref)))]
     for c in input_copies:
         c.start()
-    weight_copies = [pltpu.make_async_copy(s, d, wsem.at[i]) for i, (s, d) in enumerate(
-        ((s1_hbm, s1), (s3_hbm, s3), (s2_hbm, s2), (w1_hbm.at[0], w1), (w3_hbm.at[0], w3), (w2_hbm.at[0], w2)))]
+    expert_weights = [(w2_hbm.at[0], w2, 3)]
+    for g in range(2):
+        for cls in range(3):
+            src, dst = pl.ds((2 * cls + g) * sixth, sixth), pl.ds((3 * g + cls) * sixth, sixth)
+            expert_weights += [(w1_hbm.at[0, src], w1.at[dst], 4), (w3_hbm.at[0, src], w3.at[dst], 5)]
+    weight_copies = [local(s, d, wsem.at[i]) for s, d, i in
+                     [(s1_hbm, s1, 0), (s3_hbm, s3, 1), (s2_hbm, s2, 2)] + expert_weights]
     for c in weight_copies:
         c.start()
 
@@ -153,12 +158,6 @@
         q_slot = (sj // 32 * slots + sj // 8 % 4 * STRIDE[a2] + sj // 4 % 2 + sj % 4 * STRIDE[a3])
         for v in range(RING):
             Cs[cls, v] = dot(route_rank, as_onehot(si == q_slot + v * STRIDE[a1])).astype(BF16)
-        for d in (1, 3, 2, 0):
-            v = step_to(a1, d)
-            if d == 0:
-                Cr[cls, pos[a1]] = Cs[cls, v]
-            else:
-                remote(Cs.at[cls, v], Cr.at[cls, pos[a1]], cs, cr.at[0], me + moved(a1, v)).start()
 
     for c in weight_copies[:3]:
         c.wait()
@@ -192,21 +191,24 @@
         def _():
             wait_bytes(G.at[:, 1, 0:3], g2r.at[1])
 
-        for cls, (a1, a2, a3) in enumerate(CLASSES):
-            picks = []
-            for q in range(2):
-                d = 2 + q - p * (1 + 2 * q)
-                slot = lines[cls] + step_to(a3, d) * STRIDE[a3] + (core + e) % 2
-                picks.append(as_onehot(iota((slots, 128), 0) == slot))
+        @pl.when(g == 0)
+        def _():
+            for cls, (a1, a2, a3) in enumerate(CLASSES):
+                for q in range(2):
+                    d = 2 + q - p * (1 + 2 * q)
+                    slot = lines[cls] + step_to(a3, d) * STRIDE[a3] + (core + e) % 2
+                    pick = as_onehot(iota((slots, 128), 0) == slot)
+                    for h in range(2):
+                        val = dot(tabs[cls][h], pick)
+                        code = jnp.where(val > 0.5, val - 1.0 + src_base, -1.0)
+                        for b in range(8 * tokens // 128):
+                            Pm[p, cls, h, q * rows:(q + 1) * rows, b * 128:(b + 1) * 128] = (
+                                jnp.where(code == lane + float(b * 128), 1.0, 0.0))
+
+        for cls, (a1, a2, a3) in enumerate(CLASSES):
             outs = []
             for h in range(2):
-                for q in range(2):
-                    val = dot(tabs[cls][h], picks[q])
-                    code = jnp.where(val > 0.5, val - 1.0 + src_base, -1.0)
-                    for b in range(8 * tokens // 128):
-                        Pm[cls, h, q * rows:(q + 1) * rows, b * 128:(b + 1) * 128] = (
-                            jnp.where(code == lane + float(b * 128), 1.0, 0.0))
-                out = dot(Pm[cls, h].astype(BF16), G[cls, g, 2 * h:2 * h + 2].reshape(8 * tokens, sixth))
+                out = dot(Pm[p, cls, h].astype(BF16), G[cls, g, 2 * h:2 * h + 2].reshape(8 * tokens, sixth))
                 outs.append(out.reshape(2, CAP, 8, sixth))
             both = jnp.concatenate(outs, axis=2).astype(BF16)
             for q in range(2):
@@ -220,19 +222,27 @@
 
                     @pl.when(mine)
                     def _():
-                        local(src, dst, d3r.at[e]).start()
+                        local(src, dst, d3r.at[e, g]).start()
 
                     @pl.when(jnp.logical_not(mine))
                     def _():
-                        remote(src, dst, d3s, d3r.at[e], dev).start()
+                        remote(src, dst, d3s, d3r.at[e, g], dev).start()
                 else:
-                    remote(src, dst, d3s, d3r.at[e], dev).start()
+                    remote(src, dst, d3s, d3r.at[e, g], dev).start()
         return 0
 
     lax.fori_loop(0, 2 * RING, select, 0)
 
-    for c in weight_copies[3:]:
-        c.wait()
+    for cls, (a1, a2, a3) in enumerate(CLASSES):
+        for d in (1, 3, 2, 0):
+            v = step_to(a1, d)
+            if d == 0:
+                Cr[cls, pos[a1]] = Cs[cls, v]
+            else:
+                remote(Cs.at[cls, v], Cr.at[cls, pos[a1]], cs, cr.at[0], me + moved(a1, v)).start()
+
+    for w, i in ((w2, 3), (w1, 4), (w3, 5)):
+        wait_bytes(w, wsem.at[i])
     blk = 3 * 64
     pi, pj = iota((blk, blk), 0), iota((blk, blk), 1)
 
@@ -254,11 +264,16 @@
 
     def expert(e, _):
         half = (core + e) % 2
-        wait_bytes(R.at[:, :, 0:CAP], d3r.at[e])
         n = CAP * 64
-        xs = jnp.concatenate([permuted(to_first, cls, R[cls, g, pl.ds(half * CAP, CAP)].reshape(n, sixth))
-                              for cls in range(3) for g in range(2)], axis=1)
-        mid = (jax.nn.silu(dot(xs, w1[...])) * dot(xs, w3[...])).astype(BF16)
+        h_gate = h_up = 0.0
+        for g in range(2):
+            wait_bytes(R.at[:, g, 0:CAP], d3r.at[e, g])
+            xs = jnp.concatenate([permuted(to_first, cls, R[cls, g, pl.ds(half * CAP, CAP)].reshape(n, sixth))
+                                  for cls in range(3)], axis=1)
+            part = slice(3 * g * sixth, 3 * (g + 1) * sixth)
+            h_gate = h_gate + dot(xs, w1[part])
+            h_up = h_up + dot(xs, w3[part])
+        mid = (jax.nn.silu(h_gate) * h_up).astype(BF16)
         for cls, (a1, a2, a3) in enumerate(CLASSES):
             out = dot(mid, w2[:, cls * third:(cls + 1) * third]).astype(BF16)
             Ob[cls, pl.ds(half * CAP, CAP)] = permuted(from_first, cls, out).reshape(CAP, RING, 16, third)
@@ -357,7 +372,7 @@
         third = dim // 3
         slots = slot_expert.shape[0]
         vmem = pl.BlockSpec(memory_space=pltpu.VMEM)
-        hbm = pl.BlockSpec(memory_space=pl.ANY)
+        hbm = pl.BlockSpec(memory_space=pltpu.HBM)
         dma = pltpu.SemaphoreType.DMA
         V = pltpu.VMEM
         return pl.pallas_call(
@@ -370,7 +385,7 @@
                 V((3, 2, RING, RING, tokens, third // 2), BF16),
                 V((3, RING, RING, 16, slots), BF16),
                 V((16, slots), BF16),
-                V((3, 2, 2 * CAP * 8, 8 * tokens), F32),
+                V((2, 3, 2, 2 * CAP * 8, 8 * tokens), F32),
                 V((3, 2, 8, CAP, 16, third // 2), BF16),
                 V((3, 2, 2 * CAP, RING, 16, third // 2), BF16),
                 V((3, 2 * CAP, RING, 16, third), BF16),
@@ -383,10 +398,10 @@
                 V(w1_slots.shape[1:], BF16), V(w3_slots.shape[1:], BF16), V(w2_slots.shape[1:], BF16),
                 V(w1_shared.shape, BF16), V(w3_shared.shape, BF16), V(w2_shared.shape, BF16),
                 dma((6,)), dma((4,)), dma((9,)), dma((1,)), dma((1,)), dma((1,)), dma((2, 3)), dma((2,)), dma((1,)),
-                dma((2,)), dma((2, 3)), dma((2, 3)), dma((3,)),
+                dma((2, 2)), dma((2, 3)), dma((2, 3)), dma((3,)),
             ],
             compiler_params=pltpu.CompilerParams(collective_id=0, has_side_effects=True,
-                                                 vmem_limit_bytes=60 * 2 ** 20),
+                                                 vmem_limit_bytes=52 * 2 ** 20),
         )(x_tokens, assign.T, slot_expert.reshape(1, -1), w_router.T, w1_slots, w3_slots, w2_slots,
           w1_shared, w3_shared, w2_shared)
 

time: 79.4 us -> 77.9 us (0.981)
  Pallas kernels: 77.6 us -> 73.9 us
  local copies, waits for them, and re-layouts: 1.62 us -> 3.87 us
    pallas_call x1, Pallas kernels: 77.6 us -> 73.9 us  [device_step(): pl.pallas_call(moe_kernel, out_shape=jax.ShapeDtypeStruct((tokens, dim),...]
    unnamed x1 -> x9, local copies, waits for them, and re-layouts: 1.62 us -> 3.87 us
where the time goes in v6:
time: 77.9 us; the launch traced here: 77.7 us
  Pallas kernels  73.9 us (95%)
  local copies, waits for them, and re-layouts  3.87 us (5%)
    pallas_call x1, Pallas kernels, device_step(): pl.pallas_call(moe_kernel, out_shape=jax.ShapeDtypeStruct((tokens, dim),...  73.9 us
    unnamed x9, local copies, waits for them, and re-layouts  3.87 us

profile of v6, /device:TPU:1, one launch (start us, length us, event | category | flops | bytes accessed | tf_op | source)
XLA Modules:
  0.0 77.7 jit_solution(4756972071573489721)
XLA Ops:
  0.0 0.0 copy-start
  0.0 0.9 %copy-done = bf16[64,1536]{1,0:T(8,128)(2,1)S(1)} copy-done((bf16[64,1536]{1,0:T(8,128)(2,1)S(1)}, bf16[64,1536]{1,0:T(8,128)(2,1)}, u32[]{:S(2)}) %copy-start) | copy-done | bytes 196632
  0.9 0.0 copy-start.1
  0.9 0.9 %copy-done.1 = bf16[1536,64]{0,1:T(8,128)(2,1)S(1)} copy-done((bf16[1536,64]{0,1:T(8,128)(2,1)S(1)}, bf16[1536,64]{0,1:T(8,128)(2,1)}, u32[]{:S(2)}) %copy-start.1) | copy-done | bytes 196632
  1.9 0.0 copy-start.2
  1.9 0.7 copy-done.2
  2.5 0.0 copy-start.3
  2.5 0.7 copy-done.3
  3.2 73.9 %shard_map.100 = bf16[64,1536]{1,0:T(8,128)(2,1)S(1)} custom-call(bf16[64,1536]{1,0:T(8,128)(2,1)S(1)} %copy-done, s32[6,64]{1,0:T(8,128)S(1)} %bitcast.4, s32[1,128]{1,0:T(1,128)S(1)} %bitcast.5, bf16[64,1536]{1,0:T(8,128)(2,1)S(1)} %bitcast.3, bf16[1,1536,512]{2,1,0:T(8,128)(2,1)} %w1_hbm.1, bf16[1,1536,512]{2,1,0:T(8,128)(2,1)} %w3_hbm.1, ...), custom_call_target="tpu_custom_call" | custom-call | tf_op jit(solution)/shard_map/pallas_call | solution.py:378
  77.1 0.7 copy.12
Async XLA Ops:
  0.0 0.9 %copy-start = (bf16[64,1536]{1,0:T(8,128)(2,1)S(1)}, bf16[64,1536]{1,0:T(8,128)(2,1)}, u32[]{:S(2)}) copy-start(bf16[64,1536]{1,0:T(8,128)(2,1)} %x_hbm.1) | copy-start | bytes 589828
  0.9 0.9 %copy-start.1 = (bf16[1536,64]{0,1:T(8,128)(2,1)S(1)}, bf16[1536,64]{0,1:T(8,128)(2,1)}, u32[]{:S(2)}) copy-start(bf16[1536,64]{0,1:T(8,128)(2,1)} %param.16) | copy-start | bytes 589828
  1.9 0.7 copy-start.2
  2.5 0.7 copy-start.3

commit v7 on v6

--- a/solution.py
+++ b/solution.py
@@ -401,7 +401,7 @@
                 dma((2, 2)), dma((2, 3)), dma((2, 3)), dma((3,)),
             ],
             compiler_params=pltpu.CompilerParams(collective_id=0, has_side_effects=True,
-                                                 vmem_limit_bytes=52 * 2 ** 20),
+                                                 vmem_limit_bytes=54950 * 1024),
         )(x_tokens, assign.T, slot_expert.reshape(1, -1), w_router.T, w1_slots, w3_slots, w2_slots,
           w1_shared, w3_shared, w2_shared)
 

time: 77.9 us -> 79.5 us (1.021)
  Pallas kernels: 73.9 us -> 77.3 us
  local copies, waits for them, and re-layouts: 3.87 us -> 2.02 us
    pallas_call x1, Pallas kernels: 73.9 us -> 77.3 us  [device_step(): pl.pallas_call(moe_kernel, out_shape=jax.ShapeDtypeStruct((tokens, dim),...]
    unnamed x9 -> x5, local copies, waits for them, and re-layouts: 3.87 us -> 2.02 us
where the time goes in v7:
time: 79.5 us; the launch traced here: 79.3 us
  Pallas kernels  77.3 us (97%)
  local copies, waits for them, and re-layouts  2.02 us (3%)
    pallas_call x1, Pallas kernels, device_step(): pl.pallas_call(moe_kernel, out_shape=jax.ShapeDtypeStruct((tokens, dim),...  77.3 us
    unnamed x5, local copies, waits for them, and re-layouts  2.02 us

profile of v7, /device:TPU:1, one launch (start us, length us, event | category | flops | bytes accessed | tf_op | source)
XLA Modules:
  0.0 79.3 jit_solution(4388912459247230649)
XLA Ops:
  0.0 0.0 copy-start
  0.0 0.7 copy-done
  0.7 0.0 copy-start.1
  0.7 0.7 copy-done.1
  1.3 77.3 %shard_map.100 = bf16[64,1536]{1,0:T(8,128)(2,1)S(1)} custom-call(bf16[64,1536]{1,0:T(8,128)(2,1)} %x_hbm.1, s32[6,64]{1,0:T(8,128)S(1)} %bitcast.3, s32[1,128]{1,0:T(1,128)S(1)} %bitcast.4, bf16[64,1536]{1,0:T(8,128)(2,1)} %bitcast.5, bf16[1,1536,512]{2,1,0:T(8,128)(2,1)} %w1_hbm.1, bf16[1,1536,512]{2,1,0:T(8,128)(2,1)} %w3_hbm.1, ...), custom_call_target="tpu_custom_call" | custom-call | tf_op jit(solution)/shard_map/pallas_call | solution.py:378
  78.6 0.7 copy.12
Async XLA Ops:
  0.0 0.7 copy-start
  0.7 0.7 copy-start.1

commit v8 on v7

--- a/solution.py
+++ b/solution.py
@@ -89,8 +89,6 @@
             expert_weights += [(w1_hbm.at[0, src], w1.at[dst], 4), (w3_hbm.at[0, src], w3.at[dst], 5)]
     weight_copies = [local(s, d, wsem.at[i]) for s, d, i in
                      [(s1_hbm, s1, 0), (s3_hbm, s3, 1), (s2_hbm, s2, 2)] + expert_weights]
-    for c in weight_copies:
-        c.start()
 
     input_copies[0].wait()
     tokens = x_ref.shape[0]
@@ -131,6 +129,9 @@
             local(cols(cls, g), G.at[cls, g, pos[a2], pos[a1]], g0r.at[0]).start()
             if g == 0:
                 T[cls, pos[a2], pos[a1]] = tab[...]
+
+    for c in weight_copies:
+        c.start()
 
     gate = jax.nn.sigmoid(dot_t(x_ref[...], wr_ref[...]))
     num_experts = wr_ref.shape[0]

time: 79.5 us -> 76 us (0.956)
  Pallas kernels: 77.3 us -> 73.8 us
    pallas_call x1, Pallas kernels: 77.3 us -> 73.8 us  [device_step(): pl.pallas_call(moe_kernel, out_shape=jax.ShapeDtypeStruct((tokens, dim),...]
where the time goes in v8:
time: 76 us; the launch traced here: 75.9 us
  Pallas kernels  73.8 us (97%)
  local copies, waits for them, and re-layouts  2.02 us (3%)
    pallas_call x1, Pallas kernels, device_step(): pl.pallas_call(moe_kernel, out_shape=jax.ShapeDtypeStruct((tokens, dim),...  73.8 us
    unnamed x5, local copies, waits for them, and re-layouts  2.02 us

profile of v8, /device:TPU:1, one launch (start us, length us, event | category | flops | bytes accessed | tf_op | source)
XLA Modules:
  0.0 75.9 jit_solution(9673193745891643966)
XLA Ops:
  0.0 0.0 copy-start
  0.0 0.7 copy-done
  0.7 0.0 copy-start.1
  0.7 0.7 copy-done.1
  1.3 73.8 %shard_map.100 = bf16[64,1536]{1,0:T(8,128)(2,1)S(1)} custom-call(bf16[64,1536]{1,0:T(8,128)(2,1)} %x_hbm.1, s32[6,64]{1,0:T(8,128)S(1)} %bitcast.3, s32[1,128]{1,0:T(1,128)S(1)} %bitcast.4, bf16[64,1536]{1,0:T(8,128)(2,1)} %bitcast.5, bf16[1,1536,512]{2,1,0:T(8,128)(2,1)} %w1_hbm.1, bf16[1,1536,512]{2,1,0:T(8,128)(2,1)} %w3_hbm.1, ...), custom_call_target="tpu_custom_call" | custom-call | tf_op jit(solution)/shard_map/pallas_call | solution.py:379
  75.2 0.7 copy.12
Async XLA Ops:
  0.0 0.7 copy-start
  0.7 0.7 copy-start.1

commit v9 on v8

--- a/solution.py
+++ b/solution.py
@@ -299,23 +299,24 @@
     u2, v3 = pi // 16 % 4, pi // 4 % 4
     by_second = as_onehot(pj == pi // 64 * 64 + v3 * 16 + u2 * 4 + pi % 4)
 
-    def regroup(e, _):
+    def regroup(e):
         half = (core + e) % 2
         for cls, (a1, a2, a3) in enumerate(CLASSES):
             wait_bytes(Hb.at[cls, half], d5r.at[e, cls])
             rows_in = Hb[cls, half].reshape(CAP * 64, third)
             Z[cls, half] = jnp.concatenate([dot(by_second, rows_in[i:i + blk]).astype(BF16) for i in
                                             range(0, CAP * 64, blk)], axis=0).reshape(CAP, RING, 16, third)
-            for d in (2, 1, 3, 0):
-                v = step_to(a2, d)
-                src, dst = Z.at[cls, half, :, v], F.at[cls, half, :, pos[a2]]
-                if d == 0:
-                    local(src, dst, d6r.at[e, cls]).start()
-                else:
-                    remote(src, dst, d6s, d6r.at[e, cls], me + moved(a2, v)).start()
-        return 0
-
-    lax.fori_loop(0, 2, regroup, 0)
+            parts = [pl.ds(0, third)] if e == 0 else [pl.ds(0, sixth), pl.ds(sixth, sixth)]
+            for i, part in enumerate(parts):
+                for d in (2, 1, 3, 0):
+                    v = step_to(a2, d)
+                    src, dst = Z.at[cls, half, :, v, :, part], F.at[cls, half, :, pos[a2], :, part]
+                    if d == 0:
+                        local(src, dst, d6r.at[e + i, cls]).start()
+                    else:
+                        remote(src, dst, d6s, d6r.at[e + i, cls], me + moved(a2, v)).start()
+    for e in range(2):
+        regroup(e)
 
     wait_bytes(Cr.at[:, 0:3], cr.at[0])
 
@@ -324,42 +325,63 @@
         q = ej // 16 % 4 * 8 + half * 4 + ej // 4 % 4
         return [as_onehot(ei == q + 32 * part) for part in range(4)]
 
-    def weigh(cls, half, spread_mats, targets):
-        m = tokens * len(targets)
-        lane_pos = iota((m, 256), 1)
+    chunks = [(r0, min(4, CAP - r0)) for r0 in range(0, CAP, 4)]
+
+    def weights(cls, spread_mats, targets):
+        lane_pos = iota((tokens * len(targets), 256), 1)
         c = jnp.concatenate([Cr[cls, v] for v in targets], axis=0)
         w_exp = [dot(c, spread_mats[part]) for part in range(3)]
         source = jnp.concatenate([jnp.full((tokens, 256), v, jnp.int32) for v in targets], axis=0)
         rank_exp = jnp.where(lane_pos % 4 == source, dot(c, spread_mats[3]) - (lane_pos // 64).astype(F32), 99.0)
-        acc = jnp.zeros((3 * m, third), F32)
-        for r0 in range(0, CAP, 4):
-            k = 64 * min(4, CAP - r0)
-            hit = rank_exp == float(r0)
-            w = jnp.concatenate([jnp.where(hit, w_exp[part], 0.0) for part in range(3)], axis=0).astype(BF16)
-            acc = acc + dot(w[:, :k], F[cls, half, r0:r0 + k // 64].reshape(k, third))
-        return (acc[2 * m:] + acc[m:2 * m] + acc[:m]).reshape(len(targets), tokens, third)
-
-    mats = spreads(core)
+        return [[jnp.where(rank_exp == float(r0), w, 0.0).astype(BF16) for w in w_exp] for r0, _ in chunks]
+
+    def weigh(mats, rows_of, count, width):
+        m = tokens * count
+        acc = jnp.zeros((3 * m, width), F32)
+        for (r0, k), w in zip(chunks, mats):
+            acc = acc + dot(jnp.concatenate(w, axis=0)[:, :64 * k], rows_of(r0, k).reshape(64 * k, width))
+        return (acc[2 * m:] + acc[m:2 * m] + acc[:m]).reshape(count, tokens, width)
+
+    every = list(range(RING))
+    first, second = spreads(core), spreads(1 - core)
     for cls in range(3):
         wait_bytes(F.at[cls, core], d6r.at[0, cls])
-        U[cls] = weigh(cls, core, mats, list(range(RING)))
-    mats = spreads(1 - core)
-    for group in ((2,), (1, 3), (0,)):
-        for cls, (a1, a2, a3) in enumerate(CLASSES):
-            if group == (2,):
-                wait_bytes(F.at[cls, 1 - core], d6r.at[1, cls])
-            targets = [step_to(a1, d) for d in group]
-            part = weigh(cls, 1 - core, mats, targets)
-            for i, (d, v) in enumerate(zip(group, targets)):
-                if d == 0:
-                    A[cls, pos[a1]] = U[cls, v] + part[i]
-                else:
-                    U[cls, v] = U[cls, v] + part[i]
-                    remote(U.at[cls, v], A.at[cls, pos[a1]], d7s, d7r.at[cls], me + moved(a1, v)).start()
+        U[cls] = weigh(weights(cls, first, every), lambda r0, k: F[cls, core, r0:r0 + k], RING, third)
+
+    def place(i, part, v):
+        t = (i * 3 + part) * RING + v
+        return t // (2 * CAP), t % (2 * CAP)
+
     for cls in range(3):
-        wait_bytes(A.at[cls, 0:3], d7r.at[cls])
-        routed = (A[cls, 0] + A[cls, 1]) + (A[cls, 2] + A[cls, 3])
-        y_ref[:, cls * third:(cls + 1) * third] = (zs[:, cls * third:(cls + 1) * third] + routed).astype(BF16)
+        for i, mats in enumerate(weights(cls, second, every)):
+            for part in range(3):
+                for v in every:
+                    R[(cls,) + place(i, part, v)] = mats[part][v * tokens:(v + 1) * tokens].reshape(RING, 16, sixth)
+    for g in range(2):
+        here = slice(g * sixth, (g + 1) * sixth)
+        span = pl.ds(g * sixth, sixth)
+        for group in ((2,), (1, 3, 0)):
+            for cls, (a1, a2, a3) in enumerate(CLASSES):
+                if group == (2,):
+                    wait_bytes(F.at[cls, 1 - core, :, :, :, 0:sixth], d6r.at[1 + g, cls])
+                targets = [step_to(a1, d) for d in group]
+                mats = [[jnp.concatenate([R[(cls,) + place(i, part, v)].reshape(tokens, sixth) for v in targets], axis=0)
+                         for part in range(3)] for i in range(len(chunks))]
+                added = weigh(mats, lambda r0, k: F[cls, 1 - core, r0:r0 + k, :, :, here], len(group), sixth)
+                for i, (d, v) in enumerate(zip(group, targets)):
+                    if d == 0:
+                        A[cls, pos[a1], :, here] = U[cls, v, :, here] + added[i]
+                    else:
+                        U[cls, v, :, here] = U[cls, v, :, here] + added[i]
+                        remote(U.at[cls, v, :, span], A.at[cls, pos[a1], :, span], d7s, d7r.at[g, cls],
+                               me + moved(a1, v)).start()
+    for g in range(2):
+        for cls in range(3):
+            wait_bytes(A.at[cls, 0:3, :, 0:sixth], d7r.at[g, cls])
+            here = slice(g * sixth, (g + 1) * sixth)
+            there = slice((2 * cls + g) * sixth, (2 * cls + g + 1) * sixth)
+            routed = (A[cls, 0, :, here] + A[cls, 1, :, here]) + (A[cls, 2, :, here] + A[cls, 3, :, here])
+            y_ref[:, there] = (zs[:, there] + routed).astype(BF16)
 
     for ref, sem in ((T.at[:, 0, 0:3], t1s), (T.at[:, 0:3], t2s), (G.at[:, :, 0, 0:3], g1s), (G.at[:, :, 0:3], g2s),
                      (Cs.at[:, 0:3], cs), (Sb.at[:, :, 0:7], d3s), (Sb.at[:, :, 0:7], d5s), (Z.at[:, :, :, 0:3], d6s),
@@ -399,7 +421,7 @@
                 V(w1_slots.shape[1:], BF16), V(w3_slots.shape[1:], BF16), V(w2_slots.shape[1:], BF16),
                 V(w1_shared.shape, BF16), V(w3_shared.shape, BF16), V(w2_shared.shape, BF16),
                 dma((6,)), dma((4,)), dma((9,)), dma((1,)), dma((1,)), dma((1,)), dma((2, 3)), dma((2,)), dma((1,)),
-                dma((2, 2)), dma((2, 3)), dma((2, 3)), dma((3,)),
+                dma((2, 2)), dma((2, 3)), dma((3, 3)), dma((2, 3)),
             ],
             compiler_params=pltpu.CompilerParams(collective_id=0, has_side_effects=True,
                                                  vmem_limit_bytes=54950 * 1024),

time: 76 us -> 75 us (0.987)
  Pallas kernels: 73.8 us -> 72.8 us
    pallas_call x1, Pallas kernels: 73.8 us -> 72.8 us  [device_step(): pl.pallas_call(moe_kernel, out_shape=jax.ShapeDtypeStruct((tokens, dim),...]
where the time goes in v9:
time: 75 us; the launch traced here: 74.8 us
  Pallas kernels  72.8 us (97%)
  local copies, waits for them, and re-layouts  2.02 us (3%)
    pallas_call x1, Pallas kernels, device_step(): pl.pallas_call(moe_kernel, out_shape=jax.ShapeDtypeStruct((tokens, dim),...  72.8 us
    unnamed x5, local copies, waits for them, and re-layouts  2.02 us

profile of v9, /device:TPU:1, one launch (start us, length us, event | category | flops | bytes accessed | tf_op | source)
XLA Modules:
  0.0 74.8 jit_solution(17972048184066155406)
XLA Ops:
  0.0 0.0 copy-start
  0.0 0.7 copy-done
  0.7 0.0 copy-start.1
  0.7 0.7 copy-done.1
  1.3 72.8 %shard_map.100 = bf16[64,1536]{1,0:T(8,128)(2,1)S(1)} custom-call(bf16[64,1536]{1,0:T(8,128)(2,1)} %x_hbm.1, s32[6,64]{1,0:T(8,128)S(1)} %bitcast.3, s32[1,128]{1,0:T(1,128)S(1)} %bitcast.4, bf16[64,1536]{1,0:T(8,128)(2,1)} %bitcast.5, bf16[1,1536,512]{2,1,0:T(8,128)(2,1)} %w1_hbm.1, bf16[1,1536,512]{2,1,0:T(8,128)(2,1)} %w3_hbm.1, ...), custom_call_target="tpu_custom_call" | custom-call | tf_op jit(solution)/shard_map/pallas_call | solution.py:401
  74.1 0.7 copy.12
Async XLA Ops:
  0.0 0.7 copy-start
  0.7 0.7 copy-start.1

commit v10 on v9

--- a/solution.py
+++ b/solution.py
@@ -357,10 +357,10 @@
             for part in range(3):
                 for v in every:
                     R[(cls,) + place(i, part, v)] = mats[part][v * tokens:(v + 1) * tokens].reshape(RING, 16, sixth)
-    for g in range(2):
+    for g, groups in ((0, ((2,), (1, 3))), (1, ((2,), (1, 3), (0,))), (0, ((0,),))):
         here = slice(g * sixth, (g + 1) * sixth)
         span = pl.ds(g * sixth, sixth)
-        for group in ((2,), (1, 3, 0)):
+        for group in groups:
             for cls, (a1, a2, a3) in enumerate(CLASSES):
                 if group == (2,):
                     wait_bytes(F.at[cls, 1 - core, :, :, :, 0:sixth], d6r.at[1 + g, cls])

time: 75 us -> 74.8 us (level)
  no operation moved by 1% of the time
where the time goes in v10:
time: 74.8 us; the launch traced here: 74.6 us
  Pallas kernels  72.6 us (97%)
  local copies, waits for them, and re-layouts  2.02 us (3%)
    pallas_call x1, Pallas kernels, device_step(): pl.pallas_call(moe_kernel, out_shape=jax.ShapeDtypeStruct((tokens, dim),...  72.6 us
    unnamed x5, local copies, waits for them, and re-layouts  2.02 us

profile of v10, /device:TPU:1, one launch (start us, length us, event | category | flops | bytes accessed | tf_op | source)
XLA Modules:
  0.0 74.6 jit_solution(14412421592635389028)
XLA Ops:
  0.0 0.0 copy-start
  0.0 0.7 copy-done
  0.7 0.0 copy-start.1
  0.7 0.7 copy-done.1
  1.3 72.6 %shard_map.100 = bf16[64,1536]{1,0:T(8,128)(2,1)S(1)} custom-call(bf16[64,1536]{1,0:T(8,128)(2,1)} %x_hbm.1, s32[6,64]{1,0:T(8,128)S(1)} %bitcast.3, s32[1,128]{1,0:T(1,128)S(1)} %bitcast.4, bf16[64,1536]{1,0:T(8,128)(2,1)} %bitcast.5, bf16[1,1536,512]{2,1,0:T(8,128)(2,1)} %w1_hbm.1, bf16[1,1536,512]{2,1,0:T(8,128)(2,1)} %w3_hbm.1, ...), custom_call_target="tpu_custom_call" | custom-call | tf_op jit(solution)/shard_map/pallas_call | solution.py:401
  74.0 0.7 copy.12
Async XLA Ops:
  0.0 0.7 copy-start
  0.7 0.7 copy-start.1
